TPU v7x, 512 devices: a whole 4x8x8 slice. The times are simulated.
512 devices in a mesh: virt: 32 (over x, z), aux: 16 (over y, core).
Axes of the slice: x: 4, y: 8, z: 8, core: 2. Of those that a mesh axis runs over, the one named last changes fastest.
Arguments:
- three_index: bfloat16 [2400, 20480], P('aux', 'virt'), may hold values from -0.0625 to 0.0625
- eps_occ: float32 [20], replicated, may hold values from -1.5 to -0.5
- eps_virt: float32 [1024], replicated, may hold values from 0.3 to 3
Outputs:
- virt_energy: float32 [1024], P('virt')
- pair_energy: float32 [20, 20], replicated
All inputs are finite; a program needn't handle non-finite values.
Results may differ from a plain program's by a relative error of at most 0.0003.
Values may be sent and summed in bfloat16 or wider, within the bound.
A program may use at most 128 MiB of HBM per device.

v0:
```python
import jax
import jax.numpy as jnp
from jax import lax
from jax.sharding import Mesh
from jax.sharding import PartitionSpec as P

VIRT = ("virt_0", "virt_1")


def joined_along(tiles, dim):
    dims = list(tiles.shape[1:])
    dims[dim] *= tiles.shape[0]
    return jnp.moveaxis(tiles, 0, dim).reshape(dims)


def gather_in_order(array, axes, sequence):
    tiles = array[None]
    for k in sequence:
        tiles = lax.all_gather(tiles, axes[k], axis=0, tiled=True)
    current = [lax.axis_size(axes[k]) for k in reversed(sequence)]
    tiles = tiles.reshape(*current, *array.shape)
    turned = sorted(range(len(sequence)), key=lambda place: sequence[len(sequence) - 1 - place])
    return tiles.transpose(*turned, *range(len(sequence), tiles.ndim)).reshape(-1, *array.shape)


def whole_of(array, axes, sequence, dim):
    return joined_along(gather_in_order(array, axes, sequence), dim)


def from_everyone(array, axis):
    copies = jnp.broadcast_to(array, (lax.axis_size(axis), *array.shape))
    return lax.all_to_all(copies, axis, split_axis=0, concat_axis=0, tiled=True)


def taken_together(array, axis):
    everything = from_everyone(array, axis)
    return jnp.sum(everything, axis=0)


def together(arrays, axis):
    ends = [0]
    for a in arrays:
        ends.append(ends[-1] + a.size)
    so_far = taken_together(jnp.concatenate([a.ravel() for a in arrays]), axis)
    return tuple((so_far[b:e].reshape(a.shape) for a, b, e in zip(arrays, ends, ends[1:])))


def on_device(three_index, eps_occ, eps_virt):
    occupied = eps_occ.shape[0]
    own_width = three_index.shape[1] // occupied
    virt_count = lax.axis_size(VIRT)
    aux_place = lax.axis_index("aux")
    virt_place = lax.axis_index(VIRT)
    narrow = lax.all_to_all(three_index, "aux", split_axis=1, concat_axis=0, tiled=True)
    partner = whole_of(narrow, VIRT, (0, 1), 1)
    stride = narrow.shape[1] // occupied
    table = eps_virt.reshape(virt_count, own_width)
    eps_other = lax.dynamic_slice_in_dim(table, aux_place * stride, stride, 1).reshape(-1)
    other_width = partner.shape[1] // occupied
    partner_cube = partner.reshape(partner.shape[0], other_width, occupied)
    eps_own = lax.dynamic_slice_in_dim(eps_virt, virt_place * own_width, own_width)
    incoming = lax.all_gather(three_index, "aux", axis=0, tiled=True)
    rows = incoming.shape[0]
    left_cube = incoming.reshape(rows, own_width, occupied)
    integrals = jnp.einsum(
        "pai,pbj->iajb", left_cube, partner_cube, preferred_element_type=jnp.float32
    )
    denominator = (
        eps_occ[:, None, None, None]
        + eps_occ[None, None, :, None]
        - eps_own[None, :, None, None]
        - eps_other[None, None, None, :]
    )
    swapped = jnp.transpose(integrals, (2, 1, 0, 3))
    energy_terms = integrals * (2.0 * integrals - swapped) / denominator
    virt_local = jnp.sum(energy_terms, axis=(0, 2, 3))
    pair_local = jnp.sum(energy_terms, axis=(1, 3))
    virt_energy, pair_column = together((virt_local, pair_local), "aux")
    pair_energy = taken_together(pair_column, VIRT)
    return (virt_energy, pair_energy)


def solution(mesh):
    split = Mesh(mesh.devices.reshape(4, 8, mesh.shape["aux"]), ("virt_0", "virt_1", "aux"))
    placed = (P("aux", VIRT), P(), P())
    return jax.shard_map(
        on_device, mesh=split, in_specs=placed, out_specs=(P(VIRT), P()), check_vma=False
    )
```

profile of v0, /device:TPU:1, one launch (start us, length us, event | category | flops | bytes accessed | tf_op | source)
XLA Modules:
  0.0 213.0 jit_solution(2634388928208436110)
XLA Ops:
  7.2 0.0 all-gather.6.cloned.1.call-start
  7.2 0.7 all-gather.6.cloned.1.call-update
  7.9 0.0 all-gather.4.cloned.1.call-start
  7.9 1.1 copy.33
  9.0 22.5 %all_to_all.27 = bf16[150,16,40]{0,2,1:T(8,128)(2,1)S(1)} all-to-all(bf16[150,16,40]{0,2,1:T(8,128)(2,1)S(1)} %bitcast.42), channel_id=1, replica_groups=mesh['virt_0'=4,'virt_1'=8,'aux'=16] {'aux'}, dimensions={1} | all-to-all | bytes 384000 | tf_op jit(solution)/shard_map/all_to_all | solution.py:54
  31.6 0.1 copy.34
  31.6 0.4 broadcast_in_dim.12
  32.0 13.6 %all_gather.9 = bf16[4,2400,40]{1,2,0:T(8,128)(2,1)} all-gather(bf16[1,2400,40]{1,2,0:T(8,128)(2,1)S(1)} %broadcast_in_dim.12), channel_id=1, replica_groups=mesh['virt_0'=4,'virt_1'=8,'aux'=16] {'virt_0'}, dimensions={0}, use_global_device_ids=true | all-gather | bytes 960000 | tf_op jit(solution)/shard_map/all_gather | solution.py:19
  45.7 0.0 all-gather.4.cloned.1.call-update
  45.7 0.8 reshape.72
  46.4 0.8 dynamic_slice.6
  47.2 0.1 constant_dynamic-slice_fusion
  47.3 0.1 sub.41
  47.4 0.8 broadcast_add_fusion
  48.2 0.1 broadcast_subtract_fusion
  48.3 10.6 %all-gather.6.cloned.1.call-done = bf16[16,150,640]{2,1,0:T(8,128)(2,1)} async-done(((bf16[1,150,640]{2,1,0:T(8,128)(2,1)}), bf16[16,150,640]{2,1,0:T(8,128)(2,1)}) %all-gather.6.cloned.1.call-update) | async-done | bytes 3072016 | tf_op jit(solution)/shard_map/all_gather | solution.py:62
  58.9 8.5 %copy.36 = bf16[16,150,640]{1,0,2:T(8,128)(2,1)} copy(bf16[16,150,640]{2,1,0:T(8,128)(2,1)} %all-gather.6.cloned.1.call-done) | data formatting | bytes 6144000 | tf_op jit(solution)/shard_map/all_gather | solution.py:62
  67.4 10.8 %reshape.71 = bf16[2400,32,20]{0,2,1:T(8,128)(2,1)} reshape(bf16[16,150,640]{1,0,2:T(8,128)(2,1)} %copy.36) | data formatting | bytes 6144000 | tf_op jit(solution)/shard_map/reshape | solution.py:64
  78.2 58.4 %all-gather.4.cloned.1.call-done = bf16[32,2400,40]{1,2,0:T(8,128)(2,1)} async-done(((bf16[4,2400,40]{1,2,0:T(8,128)(2,1)}), bf16[32,2400,40]{1,2,0:T(8,128)(2,1)}) %all-gather.4.cloned.1.call-update) | async-done | bytes 6144016 | tf_op jit(solution)/shard_map/all_gather | solution.py:19
  136.6 6.0 %copy.35 = bf16[4,8,2400,40]{2,3,1,0:T(8,128)(2,1)} copy(bf16[4,8,2400,40]{2,3,0,1:T(8,128)(2,1)} %bitcast.40) | data formatting | bytes 12288000 | tf_op jit(solution)/shard_map/transpose | solution.py:23
  142.6 10.3 %reshape_reshape.3 = bf16[2400,64,20]{0,2,1:T(8,128)(2,1)} reshape(bf16[2400,32,40]{0,2,1:T(8,128)(2,1)} %bitcast.38) | data formatting | bytes 12288000 | tf_op jit(solution)/shard_map/reshape;reshape | solution.py:60
  153.0 12.8 %fusion.2 = f32[64,20,32,20]{0,2,3,1:T(8,128)S(1)} fusion(bf16[2400,64,20,1]{0,2,1,3:T(8,128)(2,1)} %bitcast.39, bf16[2400,32,20]{0,2,1:T(8,128)(2,1)} %reshape.71), kind=kOutput, calls=%fused_computation.4 | convolution fusion | flops 3932160000 | bytes 12492800 | tf_op jit(solution)/shard_map/pai,pbj->iajb/dot_general | solution.py:65
  165.8 6.5 %fusion.7 = (f32[32]{0:T(128)S(1)}, f32[20,20]{1,0:T(8,128)S(1)}) fusion(f32[64]{0:T(128)S(1)} %sub.41, f32[20,32,20]{1,2,0:T(8,128)S(1)} %broadcast_subtract_fusion, f32[64,20,32,20]{0,2,3,1:T(8,128)S(1)} %fusion.2), kind=kLoop, calls=%fused_computation.9 | loop fusion | flops 5733968 | bytes 3329984 | tf_op jit(solution)/shard_map/reduce_sum | solution.py:76
  172.3 0.1 reshape.73
  172.4 0.1 pad_maximum_fusion
  172.5 14.8 %all_to_all.28 = f32[16,1,432]{2,1,0:T(1,128)S(1)} all-to-all(f32[16,1,432]{2,1,0:T(1,128)S(1)} %broadcast_in_dim.13), channel_id=1, replica_groups=mesh['virt_0'=4,'virt_1'=8,'aux'=16] {'aux'}, dimensions={0} | all-to-all | bytes 55296 | tf_op jit(solution)/shard_map/all_to_all | solution.py:32
  187.3 0.1 slice.7
  187.4 0.1 reshape.74
  187.5 1.0 reshape.80
  188.6 6.7 %all-to-all-start.2 = ((f32[32,1,400]{2,1,0:T(1,128)}), f32[32,1,400]{2,1,0:T(1,128)S(1)}, u32[]{:S(2)}, u32[]{:S(2)}) async-start(f32[32,1,400]{2,1,0:T(1,128)} %reshape.80), calls=%async_computation.2 | async-start | bytes 131072 | tf_op jit(solution)/shard_map/all_to_all | solution.py:32
  195.2 0.5 slice.6
  195.7 8.3 %all-to-all-done.2 = f32[32,1,400]{2,1,0:T(1,128)S(1)} async-done(((f32[32,1,400]{2,1,0:T(1,128)}), f32[32,1,400]{2,1,0:T(1,128)S(1)}, u32[]{:S(2)}, u32[]{:S(2)}) %all-to-all-start.2) | async-done | bytes 51232 | tf_op jit(solution)/shard_map/all_to_all | solution.py:32
  204.1 0.5 broadcast.38
  204.6 0.8 reduce.1
  205.4 0.2 reshape.81
  205.6 0.6 reduce_sum.39
  (3 shorter events, 0.1 us)
Async XLA Ops:
  7.2 51.8 %all-gather.6.cloned.1.call-start = ((), (), s32[]{:S(2)}) async-start(), calls=%async_computation.4 | async-start | bytes 3307520 | tf_op jit(solution)/shard_map/all_gather | solution.py:62
  7.9 128.7 %all-gather.4.cloned.1.call-start = ((), (), s32[]{:S(2)}) async-start(), calls=%async_computation.3 | async-start | bytes 7004160 | tf_op jit(solution)/shard_map/all_gather | solution.py:19
  188.6 15.5 %all-to-all-start.2 = ((f32[32,1,400]{2,1,0:T(1,128)}), f32[32,1,400]{2,1,0:T(1,128)S(1)}, u32[]{:S(2)}, u32[]{:S(2)}) async-start(f32[32,1,400]{2,1,0:T(1,128)} %reshape.80), calls=%async_computation.2 | async-start | bytes 131072 | tf_op jit(solution)/shard_map/all_to_all | solution.py:32
Sparse Core Ops, SparseCore 0:
  10.1 48.8 all-gather.5
  61.0 75.5 all-gather.3
where the time goes:
time: 214 us; the launch traced here: 213 us
  waiting for transfers between devices  78.1 us (36%)
  blocking collectives  50.9 us (24%)
  local copies, waits for them, and re-layouts  41.4 us (19%)
  between operations  14.1 us (7%)
  matrix products  12.8 us (6%)
  other arithmetic  8.98 us (4%)
  starting transfers between devices  6.74 us (3%)
    all_gather x1, waiting for transfers between devices, gather_in_order(): tiles = lax.all_gather(tiles, axes[k], axis=0, tiled=True)  58.4 us
    all_to_all x1, blocking collectives, on_device(): lax.all_to_all(three_index, 'aux', split_axis=1, concat_axis=0, tiled=True)  22.5 us
    all_to_all x1, blocking collectives, from_everyone(): return lax.all_to_all(copies, axis, split_axis=0, concat_axis=0, tiled=True)  14.8 us
    all_gather x1, blocking collectives, gather_in_order(): tiles = lax.all_gather(tiles, axes[k], axis=0, tiled=True)  13.6 us
    dot_general x1, matrix products, on_device(): jnp.einsum('pai,pbj->iajb', left_cube, partner_cube, preferred_element_ty...  12.8 us
    reshape x1, local copies, waits for them, and re-layouts, on_device(): left_cube = incoming.reshape(rows, own_width, occupied)  10.8 us
    all_gather x1, waiting for transfers between devices, on_device(): incoming = lax.all_gather(three_index, 'aux', axis=0, tiled=True)  10.6 us
    another operation x1, local copies, waits for them, and re-layouts, on_device(): partner_cube = partner.reshape(partner.shape[0], other_width, occupied)  10.3 us
  transfers between devices with their start and end apart: 3, of which 3 were waited for; matrix products, arithmetic and copies ran while one was open for 11% of the time, Pallas kernels for 0%

commit v1 on v0

v1 whole, which is shorter than its diff:
```python
import jax
import jax.numpy as jnp
from jax import lax
from jax.experimental import pallas as pl
from jax.experimental.pallas import tpu as pltpu
from jax.sharding import PartitionSpec as P

MESH = pl.DeviceIdType.MESH
BF = jnp.bfloat16
F32 = jnp.float32

O = 20
NX, NY, NZ = 4, 8, 8
ROWS, KP = 150, 160
AW = 640
NB = 4
SR = NB * O
KK = NY * KP
ORDER = (
    (0, 0), (0, 7), (3, 0), (1, 7), (0, 6), (2, 0), (1, 6), (3, 6), (2, 1),
    (1, 5), (3, 7), (2, 2), (2, 5), (0, 5), (1, 4), (0, 4), (1, 3), (2, 4),
)
SLOT = {d: n for n, d in enumerate(ORDER)}
HALF = ((0, 0), (0, 4), (2, 0), (2, 4))
NBLK = len(ORDER)
NPAIR = NBLK // 2
PARENT = (
    ((1, 6), (0, 6)), ((1, 4), (1, 5)), ((3, 0), (0, 0)), ((0, 5), (1, 5)), ((2, 4), (1, 4)),
    ((2, 5), (1, 5)), ((0, 4), (1, 4)), ((2, 1), (2, 0)), ((0, 6), (0, 7)), ((2, 2), (2, 1)),
    ((0, 7), (0, 0)), ((1, 5), (1, 6)), ((2, 0), (3, 0)), ((1, 7), (0, 7)), ((3, 6), (0, 6)),
    ((3, 7), (3, 6)), ((1, 3), (1, 4)),
)
CHILDREN = {}
for _child, _parent in PARENT:
    CHILDREN.setdefault(_parent, []).append(_child)
PIECES = ((0, 256), (256, 384), (640, 384), (1024, 256))
ARRIVALS = (
    (7.8, (0, 7), 0), (7.8, (3, 0), 0), (8.9, (0, 7), 1), (8.9, (3, 0), 1), (10.6, (0, 6), 0), (10.6, (1, 7), 0),
    (10.6, (2, 0), 0), (11.7, (1, 7), 1), (11.7, (0, 7), 2), (11.7, (3, 0), 2), (12.8, (0, 6), 1), (12.8, (2, 0), 1),
    (13.4, (1, 6), 0), (13.4, (2, 1), 0), (13.9, (0, 7), 3), (13.9, (3, 0), 3), (14.5, (1, 7), 2), (15.0, (3, 6), 0),
    (15.0, (0, 6), 2), (15.6, (1, 6), 1), (15.6, (2, 1), 1), (16.1, (2, 0), 2), (16.2, (1, 5), 0), (16.7, (2, 2), 0),
    (16.7, (1, 7), 3), (17.2, (3, 6), 1), (17.3, (0, 6), 3), (17.8, (3, 7), 0), (17.8, (1, 6), 2), (18.3, (2, 0), 3),
    (18.4, (1, 5), 1), (18.9, (2, 2), 1), (19.0, (2, 5), 0), (19.4, (3, 6), 2), (19.5, (1, 4), 0), (20.0, (2, 1), 2),
    (20.1, (1, 6), 3), (20.5, (0, 5), 0), (20.6, (1, 5), 2), (21.1, (3, 7), 1), (21.2, (2, 5), 1), (21.6, (3, 6), 3),
    (21.7, (1, 4), 1), (22.2, (2, 1), 3), (22.3, (2, 4), 0), (22.7, (0, 5), 1), (22.8, (1, 3), 0), (23.3, (3, 7), 2),
    (23.4, (2, 5), 2), (23.8, (0, 4), 0), (23.9, (1, 5), 3), (24.4, (2, 2), 2), (24.5, (2, 4), 1), (24.9, (0, 5), 2),
    (25.0, (1, 4), 2), (25.5, (3, 7), 3), (26.0, (0, 4), 1), (26.1, (1, 3), 1), (26.6, (2, 2), 3), (26.7, (2, 5), 3),
    (27.1, (0, 5), 3), (27.2, (1, 4), 3), (27.8, (2, 4), 2), (28.2, (0, 4), 2), (28.3, (1, 3), 2), (30.0, (0, 4), 3),
    (30.0, (1, 3), 3), (30.0, (2, 4), 3),
)
POS = {0: 0, 1: 1, 7: 2, 2: 3, 6: 4, 3: 5, 5: 6, 4: 7}
RING = tuple((1, n, h) for n in range(3) for h in range(2)) + ((1, 3, 0),)


def split_dot(a, b):
    high = a.astype(BF)
    rest = (a - high.astype(F32)).astype(BF)
    return jnp.dot(high, b, preferred_element_type=F32) + jnp.dot(rest, b, preferred_element_type=F32)


def iota(shape, axis):
    return lax.broadcasted_iota(jnp.int32, shape, axis)


def one_hot(mask):
    return jnp.where(mask, jnp.float32(1), jnp.float32(0)).astype(BF)


def swap_quads(block):
    rows, lanes = iota((16, 128), 0) // 4, iota((16, 128), 1) // 32
    result = block
    for k in range(1, 4):
        moved = pltpu.roll(pltpu.roll(block, 4 * k, 0), 128 - 32 * k, 1)
        result = jnp.where(((rows - lanes) & 3) == k, moved, result)
    return result


def kernel(
    x_ref, eo_ref, ev_ref, virt_ref, pair_ref,
    a_buf, slab, s_in, r_buf, c_buf, c_rx, eacc, row_e, lane_e, msg, rx1, msg2, rx2,
    a_send, a_recv, s_send, s_recv, r_send, r_recv, c_send, c_recv, f_send, f_recv, g_send, g_recv,
):
    w, u = lax.axis_index("virt"), lax.axis_index("aux")
    xx, zz = w // NZ, w % NZ
    yy, core = u // 2, u % 2

    def at_plane(dx, dz):
        return (xx + dx) % NX * NZ + (zz + dz) % NZ

    def at_line(dy, dc):
        return (yy + dy) % NY * 2 + (core + dc) % 2

    barrier = pltpu.get_barrier_semaphore()
    for e in range(1, NX * NZ):
        pl.semaphore_signal(barrier, inc=1, device_id=(at_plane(e // NZ, e % NZ), u), device_id_type=MESH)
    for e in range(1, 2 * NY):
        pl.semaphore_signal(barrier, inc=1, device_id=(w, at_line(e // 2, e % 2)), device_id_type=MESH)

    pad = one_hot(iota((KP, ROWS), 0) == iota((KP, ROWS), 1))
    own = jnp.dot(pad, x_ref[...], preferred_element_type=F32).astype(BF)
    for n in range(NY):
        lane = iota((AW, 128), 1)
        source = (4 * n + lane % 4) * O + lane // 4
        pick = one_hot((iota((AW, 128), 0) == source) & (lane < SR))
        slab[n] = jnp.dot(own, pick, preferred_element_type=F32).astype(BF)
    for n in range(AW // 128):
        lane = iota((AW, 128), 1) + 128 * n
        pick = one_hot(iota((AW, 128), 0) == lane % 32 * O + lane // 32)
        a_buf[0, :, 128 * n : 128 * n + 128] = jnp.dot(own, pick, preferred_element_type=F32).astype(BF)
    pl.semaphore_wait(barrier, NX * NZ - 1 + 2 * NY - 1)

    def slab_copy(delta):
        return pltpu.make_async_remote_copy(
            src_ref=slab.at[(yy + NY - delta) % NY], dst_ref=s_in.at[POS[delta]], send_sem=s_send,
            recv_sem=s_recv.at[POS[delta]], device_id=(w, at_line(NY - delta, 0)), device_id_type=MESH,
        )

    def ring_copy(step, delta, h):
        there = (delta + step) % NY
        rows = pl.ds(h * (KP // 2), KP // 2)
        return pltpu.make_async_remote_copy(
            src_ref=a_buf.at[POS[delta], rows], dst_ref=a_buf.at[POS[there], rows], send_sem=a_send,
            recv_sem=a_recv.at[POS[there], h], device_id=(w, at_line((NY - step) % NY, 0)), device_id_type=MESH,
        )

    def tree_copy(child, parent, piece):
        lanes = pl.ds(*PIECES[piece])
        step = ((parent[0] - child[0]) % NX, (parent[1] - child[1]) % NZ)
        return pltpu.make_async_remote_copy(
            src_ref=r_buf.at[SLOT[parent], :, lanes], dst_ref=r_buf.at[SLOT[child], :, lanes], send_sem=r_send,
            recv_sem=r_recv.at[SLOT[child], piece], device_id=(at_plane(*step), u), device_id_type=MESH,
        )

    for delta in (1, 7, 2, 6, 3, 5, 4):
        slab_copy(delta).start()
    for h in range(2):
        ring_copy(1, 0, h).start()
        ring_copy(7, 0, h).start()
    s_in[0] = slab[yy]

    quad_b = iota((8, 128), 0) % 4
    for n in range(O // 2):
        top = iota((8, 128), 0) < 4
        row_e[8 * n : 8 * n + 8] = jnp.where(top, eo_ref[2 * n], eo_ref[2 * n + 1])
    own_v = jnp.zeros((8, 128), F32)
    lane32 = iota((8, 128), 1) % 32
    for a in range(32):
        own_v = jnp.where(lane32 == a, ev_ref[w * 32 + a], own_v)
    for n in range(AW // 128):
        group = iota((8, 128), 1) // 32
        occ = jnp.full((8, 128), eo_ref[4 * n], F32)
        for r in range(1, 4):
            occ = jnp.where(group == r, eo_ref[4 * n + r], occ)
        lane_e[:, 128 * n : 128 * n + 128] = occ - own_v
    eacc[...] = jnp.zeros_like(eacc)
    msg[...] = jnp.zeros_like(msg)

    eye = one_hot(iota((SR, 128), 0) == iota((SR, 128), 1))

    def turn(first, count):
        rows = s_in[first : first + count].reshape(count * KP, 128)
        return lax.dot_general(eye, rows, (((1,), (1,)), ((), ())), preferred_element_type=F32).astype(BF)

    def pass_on(block, piece):
        for child in CHILDREN.get(block, ()):
            tree_copy(child, block, piece).start()

    for pos in range(1, 4):
        slab_copy([d for d in POS if POS[d] == pos][0]).wait_recv()
    r_buf[0, :, 0:640] = turn(0, 4)
    pass_on((0, 0), 0)
    pass_on((0, 0), 1)
    for pos in range(4, 8):
        slab_copy([d for d in POS if POS[d] == pos][0]).wait_recv()
    r_buf[0, :, 640:1280] = turn(4, 4)
    pass_on((0, 0), 2)
    pass_on((0, 0), 3)

    def core_copy(p):
        return pltpu.make_async_remote_copy(
            src_ref=c_buf.at[p, 1 - core], dst_ref=c_rx.at[p], send_sem=c_send, recv_sem=c_recv.at[p],
            device_id=(w, at_line(0, 1)), device_id_type=MESH,
        )

    def multiply(p):
        rows = r_buf[2 * p : 2 * p + 2].reshape(2 * SR, KK)
        product = jnp.dot(rows, a_buf[...].reshape(KK, AW), preferred_element_type=F32)
        c_buf[p, 0] = product[:SR]
        c_buf[p, 1] = product[SR:]
        core_copy(p).start()

    def finish(p):
        core_copy(p).wait_recv()
        c_rx[p] = c_rx[p] + c_buf[p, core]
        (x0, z0), (x1, z1) = ORDER[2 * p], ORDER[2 * p + 1]
        other = at_plane(x0 + core * (x1 - x0), z0 + core * (z1 - z0))
        w0, w1 = (0.5 if d in HALF else 1.0 for d in ORDER[2 * p : 2 * p + 2])
        weight = jnp.where(core == 0, jnp.float32(w0), jnp.float32(w1))
        minus = jnp.zeros((8, 128), F32)
        for b in range(NB):
            minus = jnp.where(quad_b == b, ev_ref[other * 32 + yy * NB + b], minus)
        minus = jnp.concatenate([minus, minus], 0)
        shares = jnp.zeros((16, 128), F32)
        for q in range(5):
            rows = slice(16 * q, 16 * q + 16)
            part = row_e[rows] - minus
            for l in range(5):
                lanes = slice(128 * l, 128 * l + 128)
                value = c_rx[p, rows, lanes]
                swapped = swap_quads(c_rx[p, 16 * l : 16 * l + 16, 128 * q : 128 * q + 128])
                lane = lane_e[:, lanes]
                term = value * (2.0 * value - swapped) * (weight / (part + jnp.concatenate([lane, lane], 0)))
                eacc[rows, lanes] += term
                shares += term
        shares = shares[:8] + shares[8:]
        total = jnp.sum(shares, axis=1, keepdims=True)
        start = 64 if p < 8 else 96
        spread = jnp.where(iota((8, 128), 1) == start + yy * NB + quad_b, total, 0.0)
        line = jnp.sum(spread, axis=0, keepdims=True)
        msg[...] += jnp.where(iota((8, 128), 0) == p % 8, line, 0.0)

    events = [(t, "r", (b, piece)) for t, b, piece in ARRIVALS]
    for n in range(1, 8):
        delta, h = (n + 1) // 2, (n + 1) % 2
        events.append((8.7 + 2.2 * n, "a", (1, delta, h)))
        events.append((8.7 + 2.2 * n, "a", (7, NY - delta, h if delta < 4 else 1)))
    events.sort(key=lambda e: e[0])
    left_a = 14
    pieces = {(0, 0): 4}
    done = finished = 0

    def advance(limit):
        nonlocal done, finished
        steps = 0
        while (
            steps < limit and left_a == 0 and done < NPAIR
            and all(pieces.get(d, 0) == 4 for d in ORDER[2 * done : 2 * done + 2])
        ):
            multiply(done)
            done += 1
            if done >= 2:
                finish(finished)
                finished += 1
            steps += 1

    for _, kind, what in events:
        if kind == "a":
            step, delta, h = what
            before = (delta - step) % NY
            ring_copy(step, before, h).wait_recv()
            if delta not in (4,) and ((delta + step) % NY != 4 or h == (0 if step == 1 else 1)):
                ring_copy(step, delta, h).start()
            left_a -= 1
        else:
            block, piece = what
            parent = dict(PARENT)[block]
            tree_copy(block, parent, piece).wait_recv()
            pass_on(block, piece)
            pieces[block] = pieces.get(block, 0) + 1
        advance(1)
    advance(NPAIR)
    while finished < NPAIR:
        finish(finished)
        finished += 1

    total = eacc[...]
    lane = iota((AW, 128), 1)
    pick = one_hot((iota((AW, 128), 0) // 32 == lane % O) & (lane < 3 * O))
    summed = split_dot(total, pick)
    row, lane = iota((SR, 128), 0), iota((SR, 128), 1)
    summed = jnp.where(row // 32 == lane // O, summed, 0.0)
    fold = one_hot(iota((8, SR), 0) == iota((8, SR), 1) // 4 % 8)
    high = summed.astype(BF)
    rest = (summed - high.astype(F32)).astype(BF)
    packed = jnp.dot(fold, high, preferred_element_type=F32) + jnp.dot(fold, rest, preferred_element_type=F32)
    msg[...] += packed
    for e in range(1, NX * NZ):
        pltpu.make_async_remote_copy(
            src_ref=msg, dst_ref=rx1.at[e], send_sem=f_send, recv_sem=f_recv,
            device_id=(at_plane(e // NZ, e % NZ), u), device_id_type=MESH,
        ).start()
    own = total[:, 0:128]
    for n in range(1, 5):
        own = own + total[:, 128 * n : 128 * n + 128]
    own = jnp.sum(own, axis=0, keepdims=True)
    own = own + pltpu.roll(own, 64, 1)
    own = own + pltpu.roll(own, 32, 1)

    pltpu.make_async_copy(rx1.at[1:], rx1.at[1:], f_recv).wait()
    row, lane = iota((8, 128), 0), iota((8, 128), 1)
    pairs = msg[...]
    low = jnp.zeros((8, 128), F32)
    high = jnp.zeros((8, 128), F32)
    for e in range(NX * NZ):
        got = msg[...] if e == 0 else rx1[e]
        if e:
            pairs = pairs + got
        n = SLOT.get((e // NZ, e % NZ))
        if n is not None:
            mine = (row == n // 2 % 8) & (core == n % 2)
            if n // 2 < 8:
                low = low + jnp.where(mine, got, 0.0)
            else:
                high = high + jnp.where(mine, got, 0.0)
    low = jnp.sum(low, axis=0, keepdims=True)
    high = jnp.sum(high, axis=0, keepdims=True)
    shares = own + low + pltpu.roll(high, 96, 1)
    msg2[...] = jnp.where(lane < 64, pairs, jnp.where(row == 0, shares, 0.0))
    for e in range(1, 2 * NY):
        pltpu.make_async_remote_copy(
            src_ref=msg2, dst_ref=rx2.at[e], send_sem=g_send, recv_sem=g_recv,
            device_id=(w, at_line(NY - e // 2, e % 2)), device_id_type=MESH,
        ).start()
    pltpu.make_async_copy(rx2.at[1:], rx2.at[1:], g_recv).wait()
    total = msg2[...]
    for e in range(1, 2 * NY):
        total = total + rx2[e]
    virt_ref[...] = pltpu.roll(total, 64, 1)[0:1, 0:32]
    wide = jnp.concatenate(
        [total, pltpu.roll(total, 128 - O, 1), pltpu.roll(total, 128 - 2 * O, 1), jnp.zeros((104, 128), F32)], 0
    )
    pair_ref[...] = (wide + jnp.transpose(wide))[:O, :O]

    def drain(ref, sem):
        pltpu.make_async_copy(ref, ref, sem).wait()

    drain(s_in.at[1:], s_send)
    drain(a_buf.at[1:], a_send)
    drain(r_buf.at[1:], r_send)
    drain(c_rx, c_send)
    drain(rx1.at[1:], f_send)
    drain(rx2.at[1:], g_send)


def on_device(three_index, eps_occ, eps_virt):
    vmem, smem = pl.BlockSpec(memory_space=pltpu.VMEM), pl.BlockSpec(memory_space=pltpu.SMEM)
    dma = pltpu.SemaphoreType.DMA
    virt, pair = pl.pallas_call(
        kernel,
        out_shape=(jax.ShapeDtypeStruct((1, 32), F32), jax.ShapeDtypeStruct((O, O), F32)),
        in_specs=[vmem, smem, smem],
        out_specs=(vmem, vmem),
        scratch_shapes=[
            pltpu.VMEM((NY, KP, AW), BF),
            pltpu.VMEM((NY, KP, 128), BF),
            pltpu.VMEM((NY, KP, 128), BF),
            pltpu.VMEM((NBLK, SR, KK), BF),
            pltpu.VMEM((NPAIR, 2, SR, AW), F32),
            pltpu.VMEM((NPAIR, SR, AW), F32),
            pltpu.VMEM((SR, AW), F32),
            pltpu.VMEM((SR, 128), F32),
            pltpu.VMEM((8, AW), F32),
            pltpu.VMEM((8, 128), F32),
            pltpu.VMEM((NX * NZ, 8, 128), F32),
            pltpu.VMEM((8, 128), F32),
            pltpu.VMEM((2 * NY, 8, 128), F32),
            dma, dma((NY, 2)), dma, dma((NY,)), dma, dma((NBLK, 4)), dma, dma((NPAIR,)),
            dma, dma, dma, dma,
        ],
        compiler_params=pltpu.CompilerParams(collective_id=0, has_side_effects=True, vmem_limit_bytes=56 * 1024 * 1024),
        name="mp2",
    )(three_index, eps_occ, eps_virt)
    return virt.reshape(32), pair


def solution(mesh):
    return jax.shard_map(
        on_device, mesh=mesh, in_specs=(P("aux", "virt"), P(), P()), out_specs=(P("virt"), P()), check_vma=False
    )
```

time: 214 us -> 81.6 us (0.38)
  Pallas kernels: 0 us -> 78.3 us
  waiting for transfers between devices: 78.1 us -> 0 us
  blocking collectives: 50.9 us -> 0 us
  local copies, waits for them, and re-layouts: 41.4 us -> 2.48 us
  between operations: 14.1 us -> 0.65 us
  matrix products: 12.8 us -> 0 us
  other arithmetic: 8.98 us -> 0 us
  starting transfers between devices: 6.74 us -> 0 us
    pallas_call x0 -> x1, Pallas kernels: none -> 78.3 us  [on_device(): pl.pallas_call(kernel, out_shape=(jax.ShapeDtypeStruct((1, 32), F32), jax...]
    all_gather x2 -> x0, waiting for transfers between devices: 69.1 us -> none  [the longest x1 58.4 us: gather_in_order(): tiles = lax.all_gather(tiles, axes[k], axis=0, tiled=True)]
    all_to_all x2 -> x0, blocking collectives: 37.3 us -> none  [the longest x1 22.5 us: on_device(): lax.all_to_all(three_index, 'aux', split_axis=1, concat_axis=0, tiled=True)]
    all_gather x1 -> x0, blocking collectives: 13.6 us -> none  [gather_in_order(): tiles = lax.all_gather(tiles, axes[k], axis=0, tiled=True)]
    dot_general x1 -> x0, matrix products: 12.8 us -> none  [on_device(): jnp.einsum('pai,pbj->iajb', left_cube, partner_cube, preferred_element_ty...]
    reshape x4 -> x0, local copies, waits for them, and re-layouts: 11.7 us -> none  [the longest x1 10.8 us: on_device(): left_cube = incoming.reshape(rows, own_width, occupied)]
    another operation x1 -> x0, local copies, waits for them, and re-layouts: 10.3 us -> none  [on_device(): partner_cube = partner.reshape(partner.shape[0], other_width, occupied)]
    all_gather x1 -> x0, local copies, waits for them, and re-layouts: 8.46 us -> none  [on_device(): incoming = lax.all_gather(three_index, 'aux', axis=0, tiled=True)]
  transfers between devices with their start and end apart: 3 -> 0, of which waited for: 3 -> 0; matrix products, arithmetic and copies ran while one was open for 11% -> 0% of each run, Pallas kernels for 0% -> 0%
where the time goes in v1:
time: 81.6 us; the launch traced here: 81.4 us
  Pallas kernels  78.3 us (96%)
  local copies, waits for them, and re-layouts  2.48 us (3%)
    pallas_call x1, Pallas kernels, on_device(): pl.pallas_call(kernel, out_shape=(jax.ShapeDtypeStruct((1, 32), F32), jax...  78.3 us
    unnamed x4, local copies, waits for them, and re-layouts  2.48 us

profile of v1, /device:TPU:1, one launch (start us, length us, event | category | flops | bytes accessed | tf_op | source)
XLA Modules:
  0.0 81.4 jit_solution(2263297857179506855)
XLA Ops:
  0.6 78.3 %mp2.1 = (f32[1,32]{1,0:T(1,128)}, f32[20,20]{1,0:T(8,128)}) custom-call(bf16[150,640]{1,0:T(8,128)(2,1)} %x_ref.1, f32[20]{0:T(128)} %eo_ref.1, f32[1024]{0:T(1024)} %ev_ref.1), custom_call_target="tpu_custom_call" | custom-call | tf_op jit(solution)/shard_map/mp2/pallas_call | solution.py:338
  78.9 0.0 copy-start
  78.9 0.7 copy-done
  79.6 0.5 copy.7
  80.1 1.3 %copy.8 = f32[20,20]{1,0:T(8,128)} copy(f32[20,20]{1,0:T(8,128)} %get-tuple-element.9) | data formatting | bytes 3200
Async XLA Ops:
  78.9 0.7 copy-start

commit v2 on v1

v2 whole, which is shorter than its diff:
```python
import jax
import jax.numpy as jnp
from jax import lax
from jax.experimental import pallas as pl
from jax.experimental.pallas import tpu as pltpu
from jax.sharding import PartitionSpec as P

MESH = pl.DeviceIdType.MESH
BF = jnp.bfloat16
F32 = jnp.float32

O = 20
NX, NY, NZ = 4, 8, 8
ROWS, KP = 150, 160
AW = 640
NB = 4
SR = NB * O
KK = NY * KP
GR = 56
ORDER = (
    (0, 0), (3, 0), (3, 1), (3, 7), (0, 1), (2, 1), (3, 2), (3, 6), (0, 2),
    (3, 3), (2, 2), (2, 0), (0, 3), (3, 4), (2, 3), (3, 5), (2, 4), (0, 4),
)
SLOT = {d: n for n, d in enumerate(ORDER)}
HALF = ((0, 0), (0, 4), (2, 0), (2, 4))
NBLK = len(ORDER)
NPAIR = NBLK // 2
TREE = {
    (3, 0): (((0, 0), 6.4), ((0, 0), 8.7), ((0, 0), 9.6), ((0, 0), 10.5), ((0, 0), 11.4)),
    (3, 1): (((3, 0), 9.6), ((3, 0), 11.6), ((3, 0), 13.4), ((0, 1), 14.1), ((3, 0), 14.3)),
    (3, 7): (((3, 0), 9.3), ((3, 0), 11.6), ((3, 0), 13.4), ((3, 0), 14.3), ((3, 0), 15.2)),
    (0, 1): (((0, 0), 6.4), ((0, 0), 8.7), ((3, 1), 16.3), ((0, 0), 10.5), ((3, 1), 17.2)),
    (2, 1): (((3, 1), 13.2), ((3, 1), 15.0), ((3, 1), 16.8), ((3, 1), 17.7), ((3, 1), 18.6)),
    (3, 2): (((3, 1), 12.5), ((3, 1), 15.2), ((3, 1), 17.0), ((3, 1), 17.9), ((3, 1), 18.8)),
    (3, 6): (((3, 7), 12.5), ((3, 7), 16.1), ((3, 7), 18.8), ((3, 7), 19.7), ((3, 7), 20.6)),
    (0, 2): (((3, 2), 15.4), ((3, 2), 18.1), ((3, 2), 19.9), ((3, 2), 20.8), ((3, 2), 21.7)),
    (3, 3): (((3, 2), 16.1), ((3, 2), 19.7), ((3, 2), 20.6), ((3, 2), 21.5), ((3, 2), 22.4)),
    (2, 2): (((3, 2), 15.9), ((3, 2), 19.5), ((3, 2), 21.3), ((3, 2), 22.2), ((3, 2), 23.1)),
    (2, 0): (((2, 1), 17.9), ((3, 0), 12.3), ((2, 1), 22.4), ((2, 1), 24.2), ((2, 1), 25.1)),
    (0, 3): (((3, 3), 19.0), ((3, 3), 22.6), ((3, 3), 23.5), ((3, 3), 24.4), ((3, 3), 25.3)),
    (3, 4): (((3, 5), 23.3), ((3, 3), 23.3), ((3, 5), 28.9), ((3, 3), 25.1), ((3, 3), 26.0)),
    (2, 3): (((3, 3), 20.4), ((3, 3), 24.0), ((3, 3), 24.9), ((3, 3), 25.8), ((3, 3), 26.7)),
    (3, 5): (((3, 6), 17.0), ((3, 6), 21.5), ((3, 6), 26.0), ((3, 6), 26.9), ((3, 6), 27.8)),
    (2, 4): (((2, 3), 24.2), ((2, 3), 27.8), ((2, 3), 28.7), ((3, 4), 28.0), ((3, 4), 28.9)),
    (0, 4): (((3, 4), 26.2), ((3, 4), 27.1), ((0, 3), 26.9), ((3, 4), 28.0), ((3, 4), 28.9)),
}
PIECES = 5
PW = KK // PIECES
POS = {0: 0, 1: 1, 7: 2, 2: 3, 6: 4, 3: 5, 5: 6, 4: 7}
DELTA = {n: d for d, n in POS.items()}
NEAR = 768
A_AFTER = 5
A_START, A_STEP, LATE = 9.0, 2.2, 1.5


def hops(dx, dz, dy):
    return min(dx, NX - dx) + min(dz, NZ - dz) + min(dy, NY - dy)


PLANE = sorted(range(1, NX * NZ), key=lambda e: -hops(e // NZ, e % NZ, 0))
LINE = sorted(range(1, 2 * NY), key=lambda e: -hops(0, 0, e // 2))


def passed_on(block, piece):
    return [child for child, row in TREE.items() if row[piece][0] == block]


def program_order():
    forward, arrival = [], {((0, 0), n): 0.0 for n in range(PIECES)}
    for block, row in TREE.items():
        for piece, (_, t) in enumerate(row):
            arrival[block, piece] = t
            if passed_on(block, piece):
                forward.append((t, ("r", block, piece)))
    ring = [A_START + A_STEP * n for n in range(8)]
    for n in range(1, 7):
        delta, h = (n + 1) // 2, (n + 1) % 2
        for step, d in ((1, delta), (7, NY - delta)):
            if delta < 3 or h == (0 if step == 1 else 1):
                forward.append((ring[n], ("a", step, d, h)))
    forward.sort(key=lambda e: e[0])
    tasks = []
    for p in range(NPAIR):
        both = ORDER[2 * p : 2 * p + 2]
        first = max([ring[4]] + [arrival[b, n] for b in both for n in range(3)])
        second = max([ring[7]] + [arrival[b, n] for b in both for n in range(PIECES)])
        tasks += [[first + LATE, 0.35, ("m", p, 0)], [second + LATE, 0.25, ("m", p, 1)], [second + LATE + 1.6, 0.35, ("f", p)]]
    tasks.sort(key=lambda e: e[0])
    steps, t = [], 0.0
    while forward or tasks:
        if not tasks or forward and max(t, tasks[0][0]) + tasks[0][1] > forward[0][0]:
            when, what = forward.pop(0)
            t = max(t, when)
        else:
            ready, length, what = tasks.pop(0)
            t = max(t, ready) + length
            for task in tasks:
                if task[2] == ("f", what[1]):
                    task[0] = max(task[0], t + 1.6)
            tasks.sort(key=lambda e: e[0])
        steps.append(what)
    return steps


def split_dot(a, b):
    high = a.astype(BF)
    rest = (a - high.astype(F32)).astype(BF)
    return jnp.dot(high, b, preferred_element_type=F32) + jnp.dot(rest, b, preferred_element_type=F32)


def iota(shape, axis):
    return lax.broadcasted_iota(jnp.int32, shape, axis)


def one_hot(mask):
    return jnp.where(mask, jnp.float32(1), jnp.float32(0)).astype(BF)


def swap_quads(block):
    rows, lanes = iota((16, 128), 0) // 4, iota((16, 128), 1) // 32
    result = block
    for k in range(1, 4):
        moved = pltpu.roll(pltpu.roll(block, 4 * k, 0), 128 - 32 * k, 1)
        result = jnp.where(((rows - lanes) & 3) == k, moved, result)
    return result


def groups(block, moves):
    return [pltpu.roll(rows, m, 1) if m else rows for rows, m in zip(block, moves)]


def pack(block):
    parts = block[:GR], block[GR : 2 * GR], jnp.concatenate([block[2 * GR :], jnp.zeros((3 * GR - KP, 128), F32)], 0)
    lane = iota((GR, 128), 1)
    halves = []
    for moves in ((0, 40, 80), (88, 0, 40)):
        first, second, third = groups(parts, moves)
        halves.append(jnp.where(lane < 40, first, jnp.where(lane < 80, second, third)))
    return jnp.concatenate(halves, 0)


def unpack(block):
    low, high = block[:GR], block[GR:]
    lane = iota((GR, 128), 1)
    parts = []
    for moves in ((0, 40), (88, 0), (48, 88)):
        first, second = groups((low, high), moves)
        parts.append(jnp.where(lane < 40, first, second))
    return jnp.concatenate([parts[0], parts[1], parts[2][: KP - 2 * GR]], 0)


def kernel(
    x_ref, eo_ref, ev_ref, sum_ref,
    a_buf, slab, s_in, s_all, r_buf, c_buf, c_rx, eacc, row_e, lane_e, msg, rx1, msg2, rx2,
    a_send, a_recv, s_send, s_recv, r_send, r_recv, c_send, c_recv, f_send, f_recv, g_send, g_recv,
):
    w, u = lax.axis_index("virt"), lax.axis_index("aux")
    xx, zz = w // NZ, w % NZ
    yy, core = u // 2, u % 2

    def at_plane(dx, dz):
        return (xx + dx) % NX * NZ + (zz + dz) % NZ

    def at_line(dy, dc):
        return (yy + dy) % NY * 2 + (core + dc) % 2

    barrier = pltpu.get_barrier_semaphore()
    for e in PLANE:
        pl.semaphore_signal(barrier, inc=1, device_id=(at_plane(e // NZ, e % NZ), u), device_id_type=MESH)
    for e in LINE:
        pl.semaphore_signal(barrier, inc=1, device_id=(w, at_line(e // 2, e % 2)), device_id_type=MESH)

    pad = one_hot(iota((KP, ROWS), 0) == iota((KP, ROWS), 1))
    own = jnp.dot(pad, x_ref[...], preferred_element_type=F32).astype(BF)
    for n in range(0, NY, 2):
        lane = iota((AW, 256), 1)
        inner = lane & 127
        upper = jnp.where(inner < 40, 0, 1)
        source = (4 * n + 4 * (lane // 128) + 2 * upper + (inner & 1)) * O + (inner - 40 * upper) // 2
        pick = one_hot((iota((AW, 256), 0) == source) & (inner < SR))
        both = jnp.dot(own, pick, preferred_element_type=F32)
        slab[n] = pack(both[:, :128]).astype(BF)
        slab[n + 1] = pack(both[:, 128:]).astype(BF)
    with jax.named_scope("barrier"):
        pl.semaphore_wait(barrier, NX * NZ - 1 + 2 * NY - 1)

    def slab_copy(delta):
        return pltpu.make_async_remote_copy(
            src_ref=slab.at[(yy + NY - delta) % NY], dst_ref=s_in.at[POS[delta]], send_sem=s_send,
            recv_sem=s_recv.at[POS[delta]], device_id=(w, at_line(NY - delta, 0)), device_id_type=MESH,
        )

    def ring_copy(step, delta, h):
        there = (delta + step) % NY
        half = KP // 2
        return pltpu.make_async_remote_copy(
            src_ref=a_buf.at[pl.ds(POS[delta] * KP + h * half, half)],
            dst_ref=a_buf.at[pl.ds(POS[there] * KP + h * half, half)], send_sem=a_send,
            recv_sem=a_recv.at[POS[there], h], device_id=(w, at_line((NY - step) % NY, 0)), device_id_type=MESH,
        )

    def tree_copy(child, piece):
        parent = TREE[child][piece][0]
        lanes = pl.ds(piece * PW, PW)
        step = ((parent[0] - child[0]) % NX, (parent[1] - child[1]) % NZ)
        return pltpu.make_async_remote_copy(
            src_ref=r_buf.at[SLOT[parent], :, lanes], dst_ref=r_buf.at[SLOT[child], :, lanes], send_sem=r_send,
            recv_sem=r_recv.at[SLOT[child], piece], device_id=(at_plane(*step), u), device_id_type=MESH,
        )

    for delta in (1, 7, 2, 6, 3, 5, 4):
        slab_copy(delta).start()
    s_all[0:KP] = unpack(slab[yy].astype(F32)).astype(BF)

    for first, width in ((0, 256), (256, 256), (512, 128)):
        lane = iota((AW, width), 1) + first
        pick = one_hot(iota((AW, width), 0) == (lane & 31) * O + lane // 32)
        a_buf[0:KP, first : first + width] = jnp.dot(own, pick, preferred_element_type=F32).astype(BF)

    row = iota((SR, 128), 0)
    eye = one_hot(iota((SR, 128), 1) == (row // 2 & 1) * 40 + row // 4 * 2 + (row & 1))
    known = 0
    for piece in range(PIECES):
        need = min(((piece + 1) * PW - 1) // KP, NY - 1)
        while known < need:
            known += 1
            with jax.named_scope(f"slab_wait{known}"):
                slab_copy(DELTA[known]).wait_recv()
            s_all[known * KP : known * KP + KP] = unpack(s_in[known].astype(F32)).astype(BF)
            if known == A_AFTER:
                for h in range(2):
                    ring_copy(1, 0, h).start()
                    ring_copy(7, 0, h).start()
        lanes = slice(piece * PW, piece * PW + PW)
        turned = lax.dot_general(eye, s_all[lanes], (((1,), (1,)), ((), ())), preferred_element_type=F32)
        r_buf[0, :, lanes] = turned.astype(BF)
        for child in passed_on((0, 0), piece):
            tree_copy(child, piece).start()

    quad_b = iota((8, 128), 0) & 3
    for n in range(O // 2):
        top = iota((8, 128), 0) < 4
        row_e[8 * n : 8 * n + 8] = jnp.where(top, eo_ref[2 * n], eo_ref[2 * n + 1])
    own_v = jnp.zeros((8, 128), F32)
    lane32 = iota((8, 128), 1) & 31
    for a in range(32):
        own_v = jnp.where(lane32 == a, ev_ref[w * 32 + a], own_v)
    for n in range(AW // 128):
        group = iota((8, 128), 1) // 32
        occ = jnp.full((8, 128), eo_ref[4 * n], F32)
        for r in range(1, 4):
            occ = jnp.where(group == r, eo_ref[4 * n + r], occ)
        lane_e[:, 128 * n : 128 * n + 128] = occ - own_v
    eacc[...] = jnp.zeros_like(eacc)
    msg[...] = jnp.zeros_like(msg)

    def core_copy(p):
        return pltpu.make_async_remote_copy(
            src_ref=c_buf.at[p, 1 - core], dst_ref=c_rx.at[p], send_sem=c_send, recv_sem=c_recv.at[p],
            device_id=(w, at_line(0, 1)), device_id_type=MESH,
        )

    seen = {("r", (0, 0), n) for n in range(PIECES)} | {("a", 0, 0), ("a", 0, 1)}

    def wait_tree(block, piece):
        if ("r", block, piece) not in seen:
            seen.add(("r", block, piece))
            with jax.named_scope(f"r{block[0]}{block[1]}_{piece}"):
                tree_copy(block, piece).wait_recv()

    def wait_ring(delta, h):
        if ("a", delta, h) not in seen:
            seen.add(("a", delta, h))
            step = 1 if delta < 4 or delta == 4 and h == 0 else 7
            with jax.named_scope(f"a{delta}_{h}"):
                ring_copy(step, (delta - step) % NY, h).wait_recv()

    def multiply(p, half):
        for n in range(3) if half == 0 else range(3, PIECES):
            wait_tree(ORDER[2 * p], n)
            wait_tree(ORDER[2 * p + 1], n)
        for pos in range(5 if half == 0 else NY):
            for h in range(2):
                wait_ring(DELTA[pos], h)
        part = slice(0, NEAR) if half == 0 else slice(NEAR, KK)
        rows = r_buf[2 * p : 2 * p + 2, :, part].reshape(2 * SR, part.stop - part.start)
        product = jnp.dot(rows, a_buf[part], preferred_element_type=F32)
        if half == 0:
            c_buf[p, 0] = product[:SR]
            c_buf[p, 1] = product[SR:]
        else:
            c_buf[p, 0] += product[:SR]
            c_buf[p, 1] += product[SR:]
            core_copy(p).start()

    def finish(p):
        with jax.named_scope(f"c_wait{p}"):
            core_copy(p).wait_recv()
        c_rx[p] = c_rx[p] + c_buf[p, core]
        (x0, z0), (x1, z1) = ORDER[2 * p], ORDER[2 * p + 1]
        other = at_plane(x0 + core * (x1 - x0), z0 + core * (z1 - z0))
        w0, w1 = (0.5 if d in HALF else 1.0 for d in ORDER[2 * p : 2 * p + 2])
        weight = jnp.where(core == 0, jnp.float32(w0), jnp.float32(w1))
        minus = jnp.zeros((8, 128), F32)
        for b in range(NB):
            minus = jnp.where(quad_b == b, ev_ref[other * 32 + yy * NB + b], minus)
        minus = jnp.concatenate([minus, minus], 0)
        shares = jnp.zeros((16, 128), F32)
        for q in range(5):
            rows = slice(16 * q, 16 * q + 16)
            part = row_e[rows] - minus
            for l in range(5):
                lanes = slice(128 * l, 128 * l + 128)
                value = c_rx[p, rows, lanes]
                swapped = swap_quads(c_rx[p, 16 * l : 16 * l + 16, 128 * q : 128 * q + 128])
                lane = lane_e[:, lanes]
                term = value * (2.0 * value - swapped) * (weight / (part + jnp.concatenate([lane, lane], 0)))
                eacc[rows, lanes] += term
                shares += term
        shares = shares[:8] + shares[8:]
        total = jnp.sum(shares[:4] + shares[4:], axis=1, keepdims=True)
        msg[...] += jnp.where(iota((4, 128), 1) == 100 + p, total, 0.0)

    for step in program_order():
        if step[0] == "a":
            _, way, delta, h = step
            wait_ring(delta, h)
            ring_copy(way, delta, h).start()
        elif step[0] == "r":
            _, block, piece = step
            wait_tree(block, piece)
            for child in passed_on(block, piece):
                tree_copy(child, piece).start()
        else:
            with jax.named_scope("_".join(map(str, step))):
                multiply(*step[1:]) if step[0] == "m" else finish(*step[1:])

    total = eacc[...]
    lane = iota((AW, 128), 1)
    pick = one_hot((iota((AW, 128), 0) // 32 == lane % O) & (lane < 5 * O))
    summed = split_dot(total, pick)
    row, lane = iota((SR, 128), 0), iota((SR, 128), 1)
    summed = jnp.where(row // 16 == lane // O, summed, 0.0)
    fold = one_hot(iota((8, SR), 0) == (iota((8, SR), 1) // 4 & 3))
    high = summed.astype(BF)
    rest = (summed - high.astype(F32)).astype(BF)
    packed = jnp.dot(fold, high, preferred_element_type=F32) + jnp.dot(fold, rest, preferred_element_type=F32)
    msg[...] += packed[:4]
    for e in PLANE:
        pltpu.make_async_remote_copy(
            src_ref=msg, dst_ref=rx1.at[e], send_sem=f_send, recv_sem=f_recv,
            device_id=(at_plane(e // NZ, e % NZ), u), device_id_type=MESH,
        ).start()
    own = total[:, 0:128]
    for n in range(1, 5):
        own = own + total[:, 128 * n : 128 * n + 128]
    own = jnp.sum(own, axis=0, keepdims=True)
    own = own + pltpu.roll(own, 64, 1)
    own = own + pltpu.roll(own, 32, 1)
    row, lane = iota((4, 128), 0), iota((4, 128), 1)
    tail = jnp.zeros((4, 128), F32)
    for r in range(4):
        tail = jnp.where(row == r, pltpu.roll(own, 100 - 8 * r, 1), tail)

    with jax.named_scope("f_wait"):
        pltpu.make_async_copy(rx1.at[1:], rx1.at[1:], f_recv).wait()
    pairs = msg[...]
    theirs = jnp.zeros((4, 128), F32)
    for e in range(NX * NZ):
        got = msg[...] if e == 0 else rx1[e]
        if e:
            pairs = pairs + got
        n = SLOT.get((e // NZ, e % NZ))
        if n is not None:
            theirs = theirs + jnp.where((lane == 100 + n // 2) & (core == n % 2), got, 0.0)
    theirs = jnp.sum(theirs, axis=1, keepdims=True)
    theirs = jnp.where(lane == 100 + (yy & 1) * NB + row, theirs, 0.0)
    theirs = jnp.sum(theirs, axis=0, keepdims=True)
    tail = tail + jnp.where(row == yy // 2, theirs, 0.0)
    msg2[...] = jnp.where(lane < 100, pairs, tail)
    for e in LINE:
        pltpu.make_async_remote_copy(
            src_ref=msg2, dst_ref=rx2.at[e], send_sem=g_send, recv_sem=g_recv,
            device_id=(w, at_line(NY - e // 2, e % 2)), device_id_type=MESH,
        ).start()
    with jax.named_scope("g_wait"):
        pltpu.make_async_copy(rx2.at[1:], rx2.at[1:], g_recv).wait()
    total = msg2[...]
    for e in range(1, 2 * NY):
        total = total + rx2[e]
    sum_ref[...] = total

    def drain(ref, sem):
        pltpu.make_async_copy(ref, ref, sem).wait()

    drain(s_in.at[1:], s_send)
    drain(a_buf.at[KP:], a_send)
    drain(r_buf.at[1:], r_send)
    drain(c_rx, c_send)
    drain(rx1.at[1:], f_send)
    drain(rx2.at[1:], g_send)


def open_sums(sum_ref, virt_ref, pair_ref, square):
    total = sum_ref[...]
    row, lane = iota((4, 128), 0), iota((4, 128), 1)
    line = jnp.zeros((4, 128), F32)
    for r in range(4):
        line = jnp.where((row == r) & (lane // 8 == r), pltpu.roll(total, 28 + 8 * r, 1), line)
    virt_ref[...] = jnp.sum(line, axis=0)[:32]
    square[...] = jnp.zeros_like(square)
    for q in range(5):
        square[4 * q : 4 * q + 4] = pltpu.roll(total, (128 - O * q) % 128, 1)
    wide = square[...]
    pair_ref[...] = (wide + jnp.transpose(wide))[:O, :O]


def on_device(three_index, eps_occ, eps_virt):
    vmem, smem = pl.BlockSpec(memory_space=pltpu.VMEM), pl.BlockSpec(memory_space=pltpu.SMEM)
    dma = pltpu.SemaphoreType.DMA
    sums = pl.pallas_call(
        kernel,
        out_shape=jax.ShapeDtypeStruct((4, 128), F32),
        in_specs=[vmem, smem, smem],
        out_specs=vmem,
        scratch_shapes=[
            pltpu.VMEM((KK, AW), BF),
            pltpu.VMEM((NY, 2 * GR, 128), BF),
            pltpu.VMEM((NY, 2 * GR, 128), BF),
            pltpu.VMEM((KK, 128), BF),
            pltpu.VMEM((NBLK, SR, KK), BF),
            pltpu.VMEM((NPAIR, 2, SR, AW), F32),
            pltpu.VMEM((NPAIR, SR, AW), F32),
            pltpu.VMEM((SR, AW), F32),
            pltpu.VMEM((SR, 128), F32),
            pltpu.VMEM((8, AW), F32),
            pltpu.VMEM((4, 128), F32),
            pltpu.VMEM((NX * NZ, 4, 128), F32),
            pltpu.VMEM((4, 128), F32),
            pltpu.VMEM((2 * NY, 4, 128), F32),
            dma, dma((NY, 2)), dma, dma((NY,)), dma, dma((NBLK, PIECES)), dma, dma((NPAIR,)),
            dma, dma, dma, dma,
        ],
        compiler_params=pltpu.CompilerParams(collective_id=0, has_side_effects=True, vmem_limit_bytes=56 * 1024 * 1024),
        name="mp2",
    )(three_index, eps_occ, eps_virt)
    return pl.pallas_call(
        open_sums,
        out_shape=(jax.ShapeDtypeStruct((32,), F32), jax.ShapeDtypeStruct((O, O), F32)),
        in_specs=[vmem],
        out_specs=(vmem, vmem),
        scratch_shapes=[pltpu.VMEM((128, 128), F32)],
        name="sums",
    )(sums)


def solution(mesh):
    return jax.shard_map(
        on_device, mesh=mesh, in_specs=(P("aux", "virt"), P(), P()), out_specs=(P("virt"), P()), check_vma=False
    )
```

time: 81.6 us -> 68.8 us (0.84)
  Pallas kernels: 78.3 us -> 68 us
  local copies, waits for them, and re-layouts: 2.48 us -> 0 us
    pallas_call x1 -> x2, Pallas kernels: 78.3 us -> 68 us  [the longest x1 66.5 us: on_device(): pl.pallas_call(kernel, out_shape=jax.ShapeDtypeStruct((4, 128), F32), in_...]
    unnamed x4 -> x0, local copies, waits for them, and re-layouts: 2.48 us -> none
where the time goes in v2:
time: 68.8 us; the launch traced here: 68.6 us
  Pallas kernels  68 us (99%)
    pallas_call x1, Pallas kernels, on_device(): pl.pallas_call(kernel, out_shape=jax.ShapeDtypeStruct((4, 128), F32), in_...  66.5 us
    pallas_call x1, Pallas kernels, on_device(): pl.pallas_call(open_sums, out_shape=(jax.ShapeDtypeStruct((32,), F32), ja...  1.43 us

profile of v2, /device:TPU:1, one launch (start us, length us, event | category | flops | bytes accessed | tf_op | source)
XLA Modules:
  0.0 68.6 jit_solution(14436430327575411217)
XLA Ops:
  0.6 66.5 %mp2.1.sum_ref = f32[4,128]{1,0:T(4,128)} custom-call(bf16[150,640]{1,0:T(8,128)(2,1)} %x_ref.1, f32[20]{0:T(128)} %eo_ref.1, f32[1024]{0:T(1024)} %ev_ref.1), custom_call_target="tpu_custom_call" | custom-call | tf_op jit(solution)/shard_map/mp2/pallas_call | solution.py:421
  67.2 1.4 %sums.1 = (f32[32]{0:T(128)}, f32[20,20]{1,0:T(8,128)}) custom-call(f32[4,128]{1,0:T(4,128)} %mp2.1.sum_ref), custom_call_target="tpu_custom_call" | custom-call | tf_op jit(solution)/shard_map/sums/pallas_call | solution.py:447

commit v3 on v2

--- a/solution.py
+++ b/solution.py
@@ -18,39 +18,46 @@
 KK = NY * KP
 GR = 56
 ORDER = (
-    (0, 0), (3, 0), (3, 1), (3, 7), (0, 1), (2, 1), (3, 2), (3, 6), (0, 2),
-    (3, 3), (2, 2), (2, 0), (0, 3), (3, 4), (2, 3), (3, 5), (2, 4), (0, 4),
+    (0, 0), (1, 0), (0, 1), (3, 1), (2, 0), (0, 2), (2, 7), (3, 2), (0, 3),
+    (2, 6), (3, 7), (3, 3), (0, 4), (2, 5), (3, 6), (3, 4), (2, 4), (3, 5),
 )
 SLOT = {d: n for n, d in enumerate(ORDER)}
 HALF = ((0, 0), (0, 4), (2, 0), (2, 4))
 NBLK = len(ORDER)
 NPAIR = NBLK // 2
 TREE = {
-    (3, 0): (((0, 0), 6.4), ((0, 0), 8.7), ((0, 0), 9.6), ((0, 0), 10.5), ((0, 0), 11.4)),
-    (3, 1): (((3, 0), 9.6), ((3, 0), 11.6), ((3, 0), 13.4), ((0, 1), 14.1), ((3, 0), 14.3)),
-    (3, 7): (((3, 0), 9.3), ((3, 0), 11.6), ((3, 0), 13.4), ((3, 0), 14.3), ((3, 0), 15.2)),
-    (0, 1): (((0, 0), 6.4), ((0, 0), 8.7), ((3, 1), 16.3), ((0, 0), 10.5), ((3, 1), 17.2)),
-    (2, 1): (((3, 1), 13.2), ((3, 1), 15.0), ((3, 1), 16.8), ((3, 1), 17.7), ((3, 1), 18.6)),
-    (3, 2): (((3, 1), 12.5), ((3, 1), 15.2), ((3, 1), 17.0), ((3, 1), 17.9), ((3, 1), 18.8)),
-    (3, 6): (((3, 7), 12.5), ((3, 7), 16.1), ((3, 7), 18.8), ((3, 7), 19.7), ((3, 7), 20.6)),
-    (0, 2): (((3, 2), 15.4), ((3, 2), 18.1), ((3, 2), 19.9), ((3, 2), 20.8), ((3, 2), 21.7)),
-    (3, 3): (((3, 2), 16.1), ((3, 2), 19.7), ((3, 2), 20.6), ((3, 2), 21.5), ((3, 2), 22.4)),
-    (2, 2): (((3, 2), 15.9), ((3, 2), 19.5), ((3, 2), 21.3), ((3, 2), 22.2), ((3, 2), 23.1)),
-    (2, 0): (((2, 1), 17.9), ((3, 0), 12.3), ((2, 1), 22.4), ((2, 1), 24.2), ((2, 1), 25.1)),
-    (0, 3): (((3, 3), 19.0), ((3, 3), 22.6), ((3, 3), 23.5), ((3, 3), 24.4), ((3, 3), 25.3)),
-    (3, 4): (((3, 5), 23.3), ((3, 3), 23.3), ((3, 5), 28.9), ((3, 3), 25.1), ((3, 3), 26.0)),
-    (2, 3): (((3, 3), 20.4), ((3, 3), 24.0), ((3, 3), 24.9), ((3, 3), 25.8), ((3, 3), 26.7)),
-    (3, 5): (((3, 6), 17.0), ((3, 6), 21.5), ((3, 6), 26.0), ((3, 6), 26.9), ((3, 6), 27.8)),
-    (2, 4): (((2, 3), 24.2), ((2, 3), 27.8), ((2, 3), 28.7), ((3, 4), 28.0), ((3, 4), 28.9)),
-    (0, 4): (((3, 4), 26.2), ((3, 4), 27.1), ((0, 3), 26.9), ((3, 4), 28.0), ((3, 4), 28.9)),
+    (1, 0): (((0, 0), 6.8), ((0, 0), 9.2), ((0, 0), 11.0), ((0, 0), 13.2), ((0, 0), 14.1)),
+    (0, 1): (((0, 0), 6.8), ((0, 0), 9.2), ((0, 0), 11.0), ((0, 0), 13.2), ((0, 0), 15.0)),
+    (3, 1): (((3, 2), 17.2), ((0, 1), 12.3), ((0, 1), 14.1), ((0, 1), 16.3), ((0, 1), 18.1)),
+    (2, 0): (((1, 0), 10.1), ((1, 0), 12.3), ((1, 0), 15.0), ((1, 0), 16.3), ((1, 0), 18.1)),
+    (0, 2): (((0, 1), 10.1), ((0, 1), 12.3), ((0, 1), 15.9), ((0, 1), 17.7), ((0, 1), 18.6)),
+    (2, 7): (((2, 0), 13.2), ((2, 0), 15.4), ((2, 0), 18.1), ((2, 0), 19.9), ((2, 0), 21.2)),
+    (3, 2): (((0, 2), 13.2), ((0, 2), 15.4), ((0, 2), 19.0), ((0, 2), 20.8), ((0, 2), 21.7)),
+    (0, 3): (((0, 2), 14.1), ((0, 2), 16.8), ((0, 2), 19.5), ((0, 2), 21.3), ((0, 2), 22.2)),
+    (2, 6): (((2, 7), 16.3), ((2, 7), 19.0), ((2, 7), 22.1), ((2, 7), 23.0), ((2, 7), 24.3)),
+    (3, 7): (((2, 7), 17.2), ((2, 7), 19.0), ((2, 7), 21.2), ((2, 7), 23.0), ((2, 7), 24.8)),
+    (3, 3): (((0, 3), 17.2), ((0, 3), 19.9), ((0, 3), 22.6), ((0, 3), 24.4), ((0, 3), 25.3)),
+    (0, 4): (((3, 4), 23.9), ((3, 4), 27.5), ((0, 3), 23.1), ((0, 3), 25.8), ((0, 3), 26.7)),
+    (2, 5): (((3, 5), 28.0), ((2, 4), 30.2), ((2, 6), 25.2), ((2, 6), 26.1), ((2, 6), 27.4)),
+    (3, 6): (((2, 6), 19.9), ((2, 6), 22.1), ((2, 6), 25.7), ((2, 6), 26.6), ((3, 7), 28.3)),
+    (3, 4): (((3, 3), 20.4), ((3, 3), 24.0), ((0, 4), 26.2), ((0, 4), 28.9), ((3, 3), 28.5)),
+    (2, 4): (((3, 4), 23.5), ((3, 4), 27.1), ((3, 4), 29.8), ((2, 5), 29.2), ((2, 5), 30.5)),
+    (3, 5): (((3, 4), 24.9), ((3, 4), 27.6), ((2, 5), 28.4), ((2, 5), 29.3), ((2, 5), 30.5)),
 }
-PIECES = 5
-PW = KK // PIECES
+BOUNDS = (0, 256, 512, 768, 1024, 1280)
+PIECES = len(BOUNDS) - 1
 POS = {0: 0, 1: 1, 7: 2, 2: 3, 6: 4, 3: 5, 5: 6, 4: 7}
 DELTA = {n: d for d, n in POS.items()}
-NEAR = 768
-A_AFTER = 5
-A_START, A_STEP, LATE = 9.0, 2.2, 1.5
+PARTS = (0, 768, KK)
+A_AFTER = 3
+A_PARTS = 5
+LATE, SLACK, GAP = 0.7, 0.5, 3.5
+SLABS = (0.0, 3.3, 4.2, 5.8, 6.8, 8.5, 8.9, 9.8)
+
+RING = {
+    1: (8.9, 9.8, 10.7, 11.6, 12.5, 13.4, 14.3, 15.2, 16.1, 17.0, 17.9, 18.8, 19.7, 20.6, 21.5, 22.4, 23.3, 24.2),
+    7: (8.9, 9.8, 10.7, 11.6, 12.5, 13.4, 14.3, 15.2, 16.1, 17.0, 17.9, 18.8, 19.7, 20.6, 21.5, 22.4, 23.3),
+}
 
 
 def hops(dx, dz, dy):
@@ -63,6 +70,20 @@
 
 def passed_on(block, piece):
     return [child for child, row in TREE.items() if row[piece][0] == block]
+
+
+def ring_pieces(step):
+    last = range(3) if step == 1 else range(3, A_PARTS)
+    return [(step * n % NY, h) for n in range(1, 4) for h in range(A_PARTS)] + [(4, h) for h in last]
+
+
+def ring_goes_on(step, delta, h):
+    return ((delta + step) % NY, h) in ring_pieces(step)
+
+
+def part_needs(first, last):
+    pieces = [m for m in range(PIECES) if BOUNDS[m] < last and BOUNDS[m + 1] > first]
+    return pieces, range(first // KP, (last - 1) // KP + 1)
 
 
 def program_order():
@@ -72,31 +93,40 @@
             arrival[block, piece] = t
             if passed_on(block, piece):
                 forward.append((t, ("r", block, piece)))
-    ring = [A_START + A_STEP * n for n in range(8)]
-    for n in range(1, 7):
-        delta, h = (n + 1) // 2, (n + 1) % 2
-        for step, d in ((1, delta), (7, NY - delta)):
-            if delta < 3 or h == (0 if step == 1 else 1):
-                forward.append((ring[n], ("a", step, d, h)))
+    forward += [(t, ("s", pos)) for pos, t in enumerate(SLABS) if pos]
+    rings = {}
+    for step, times in RING.items():
+        for (delta, h), t in zip(ring_pieces(step), times):
+            rings[delta, h] = t
+            if ring_goes_on(step, delta, h):
+                forward.append((t, ("a", step, delta, h)))
     forward.sort(key=lambda e: e[0])
-    tasks = []
+    tasks = [[0.0, 0.25, ("d", p)] for p in range(NPAIR)]
+    last = max(rings.values())
     for p in range(NPAIR):
         both = ORDER[2 * p : 2 * p + 2]
-        first = max([ring[4]] + [arrival[b, n] for b in both for n in range(3)])
-        second = max([ring[7]] + [arrival[b, n] for b in both for n in range(PIECES)])
-        tasks += [[first + LATE, 0.35, ("m", p, 0)], [second + LATE, 0.25, ("m", p, 1)], [second + LATE + 1.6, 0.35, ("f", p)]]
+        early = max(arrival[b, m] for b in both for m in range(PIECES)) < last - 1.0
+        bounds = PARTS if early else (0, KK)
+        ready = 0.0
+        for a, b in zip(bounds, bounds[1:]):
+            pieces, chunks = part_needs(a, b)
+            times = [arrival[d, m] for d in both for m in pieces]
+            times += [rings[DELTA[m], h] for m in chunks if m for h in range(A_PARTS)]
+            ready = max([ready] + times)
+            tasks.append([ready + LATE, 0.2 + 0.25 * (b - a) / KK, ("m", p, a, b)])
+        tasks.append([ready + LATE + GAP, 0.25, ("f", p)])
     tasks.sort(key=lambda e: e[0])
     steps, t = [], 0.0
     while forward or tasks:
-        if not tasks or forward and max(t, tasks[0][0]) + tasks[0][1] > forward[0][0]:
+        if not tasks or forward and max(t, tasks[0][0]) + tasks[0][1] > forward[0][0] + SLACK:
             when, what = forward.pop(0)
             t = max(t, when)
         else:
             ready, length, what = tasks.pop(0)
             t = max(t, ready) + length
             for task in tasks:
-                if task[2] == ("f", what[1]):
-                    task[0] = max(task[0], t + 1.6)
+                if what[0] == "m" and task[2] == ("f", what[1]):
+                    task[0] = max(task[0], t + GAP)
             tasks.sort(key=lambda e: e[0])
         steps.append(what)
     return steps
@@ -117,12 +147,17 @@
 
 
 def swap_quads(block):
-    rows, lanes = iota((16, 128), 0) // 4, iota((16, 128), 1) // 32
-    result = block
-    for k in range(1, 4):
-        moved = pltpu.roll(pltpu.roll(block, 4 * k, 0), 128 - 32 * k, 1)
-        result = jnp.where(((rows - lanes) & 3) == k, moved, result)
-    return result
+    row, lane = iota((8, 128), 0) // 4, iota((8, 128), 1) // 32
+    far = lane // 2
+    top = jnp.where(far == 0, block[:8], pltpu.roll(block[8:], 64, 1))
+    bottom = jnp.where(far == 1, block[8:], pltpu.roll(block[:8], 64, 1))
+    near = lane & 1
+    result = []
+    for part in (top, bottom):
+        turned = pltpu.roll(part, 4, 0)
+        moved = jnp.where(near == 1, pltpu.roll(turned, 32, 1), pltpu.roll(turned, 96, 1))
+        result.append(jnp.where(near == row, part, moved))
+    return jnp.concatenate(result, 0)
 
 
 def groups(block, moves):
@@ -151,7 +186,7 @@
 
 def kernel(
     x_ref, eo_ref, ev_ref, sum_ref,
-    a_buf, slab, s_in, s_all, r_buf, c_buf, c_rx, eacc, row_e, lane_e, msg, rx1, msg2, rx2,
+    a_buf, slab, s_in, s_all, r_buf, c_buf, c_rx, factor, eacc, row_e, lane_e, msg, rx1, msg2, rx2,
     a_send, a_recv, s_send, s_recv, r_send, r_recv, c_send, c_recv, f_send, f_recv, g_send, g_recv,
 ):
     w, u = lax.axis_index("virt"), lax.axis_index("aux")
@@ -192,16 +227,16 @@
 
     def ring_copy(step, delta, h):
         there = (delta + step) % NY
-        half = KP // 2
+        part = KP // A_PARTS
         return pltpu.make_async_remote_copy(
-            src_ref=a_buf.at[pl.ds(POS[delta] * KP + h * half, half)],
-            dst_ref=a_buf.at[pl.ds(POS[there] * KP + h * half, half)], send_sem=a_send,
+            src_ref=a_buf.at[pl.ds(POS[delta] * KP + h * part, part)],
+            dst_ref=a_buf.at[pl.ds(POS[there] * KP + h * part, part)], send_sem=a_send,
             recv_sem=a_recv.at[POS[there], h], device_id=(w, at_line((NY - step) % NY, 0)), device_id_type=MESH,
         )
 
     def tree_copy(child, piece):
         parent = TREE[child][piece][0]
-        lanes = pl.ds(piece * PW, PW)
+        lanes = pl.ds(BOUNDS[piece], BOUNDS[piece + 1] - BOUNDS[piece])
         step = ((parent[0] - child[0]) % NX, (parent[1] - child[1]) % NZ)
         return pltpu.make_async_remote_copy(
             src_ref=r_buf.at[SLOT[parent], :, lanes], dst_ref=r_buf.at[SLOT[child], :, lanes], send_sem=r_send,
@@ -212,30 +247,34 @@
         slab_copy(delta).start()
     s_all[0:KP] = unpack(slab[yy].astype(F32)).astype(BF)
 
+    row = iota((SR, 128), 0)
+    eye = one_hot(iota((SR, 128), 1) == (row // 2 & 1) * 40 + row // 4 * 2 + (row & 1))
+    def own_piece(piece):
+        lanes = slice(BOUNDS[piece], BOUNDS[piece + 1])
+        turned = lax.dot_general(eye, s_all[lanes], (((1,), (1,)), ((), ())), preferred_element_type=F32)
+        r_buf[0, :, lanes] = turned.astype(BF)
+        for child in passed_on((0, 0), piece):
+            tree_copy(child, piece).start()
+
+    def take_slab(pos):
+        with jax.named_scope(f"slab_wait{pos}"):
+            slab_copy(DELTA[pos]).wait_recv()
+        s_all[pos * KP : pos * KP + KP] = unpack(s_in[pos].astype(F32)).astype(BF)
+        for piece in range(PIECES):
+            if (BOUNDS[piece + 1] - 1) // KP == pos:
+                own_piece(piece)
+        if pos == A_AFTER:
+            for h in range(A_PARTS):
+                ring_copy(1, 0, h).start()
+                ring_copy(7, 0, h).start()
+
+    if BOUNDS[1] <= KP:
+        own_piece(0)
+
     for first, width in ((0, 256), (256, 256), (512, 128)):
         lane = iota((AW, width), 1) + first
         pick = one_hot(iota((AW, width), 0) == (lane & 31) * O + lane // 32)
         a_buf[0:KP, first : first + width] = jnp.dot(own, pick, preferred_element_type=F32).astype(BF)
-
-    row = iota((SR, 128), 0)
-    eye = one_hot(iota((SR, 128), 1) == (row // 2 & 1) * 40 + row // 4 * 2 + (row & 1))
-    known = 0
-    for piece in range(PIECES):
-        need = min(((piece + 1) * PW - 1) // KP, NY - 1)
-        while known < need:
-            known += 1
-            with jax.named_scope(f"slab_wait{known}"):
-                slab_copy(DELTA[known]).wait_recv()
-            s_all[known * KP : known * KP + KP] = unpack(s_in[known].astype(F32)).astype(BF)
-            if known == A_AFTER:
-                for h in range(2):
-                    ring_copy(1, 0, h).start()
-                    ring_copy(7, 0, h).start()
-        lanes = slice(piece * PW, piece * PW + PW)
-        turned = lax.dot_general(eye, s_all[lanes], (((1,), (1,)), ((), ())), preferred_element_type=F32)
-        r_buf[0, :, lanes] = turned.astype(BF)
-        for child in passed_on((0, 0), piece):
-            tree_copy(child, piece).start()
 
     quad_b = iota((8, 128), 0) & 3
     for n in range(O // 2):
@@ -260,7 +299,7 @@
             device_id=(w, at_line(0, 1)), device_id_type=MESH,
         )
 
-    seen = {("r", (0, 0), n) for n in range(PIECES)} | {("a", 0, 0), ("a", 0, 1)}
+    seen = {("r", (0, 0), n) for n in range(PIECES)} | {("a", 0, h) for h in range(A_PARTS)}
 
     def wait_tree(block, piece):
         if ("r", block, piece) not in seen:
@@ -271,32 +310,31 @@
     def wait_ring(delta, h):
         if ("a", delta, h) not in seen:
             seen.add(("a", delta, h))
-            step = 1 if delta < 4 or delta == 4 and h == 0 else 7
+            step = 1 if (delta, h) in ring_pieces(1) else 7
             with jax.named_scope(f"a{delta}_{h}"):
                 ring_copy(step, (delta - step) % NY, h).wait_recv()
 
-    def multiply(p, half):
-        for n in range(3) if half == 0 else range(3, PIECES):
-            wait_tree(ORDER[2 * p], n)
-            wait_tree(ORDER[2 * p + 1], n)
-        for pos in range(5 if half == 0 else NY):
-            for h in range(2):
-                wait_ring(DELTA[pos], h)
-        part = slice(0, NEAR) if half == 0 else slice(NEAR, KK)
-        rows = r_buf[2 * p : 2 * p + 2, :, part].reshape(2 * SR, part.stop - part.start)
+    def multiply(p, first, last):
+        pieces, chunks = part_needs(first, last)
+        for m in pieces:
+            wait_tree(ORDER[2 * p], m)
+            wait_tree(ORDER[2 * p + 1], m)
+        for m in chunks:
+            for h in range(A_PARTS):
+                wait_ring(DELTA[m], h)
+        part = slice(first, last)
+        rows = r_buf[2 * p : 2 * p + 2, :, part].reshape(2 * SR, last - first)
         product = jnp.dot(rows, a_buf[part], preferred_element_type=F32)
-        if half == 0:
+        if first == 0:
             c_buf[p, 0] = product[:SR]
             c_buf[p, 1] = product[SR:]
         else:
             c_buf[p, 0] += product[:SR]
             c_buf[p, 1] += product[SR:]
+        if last == KK:
             core_copy(p).start()
 
-    def finish(p):
-        with jax.named_scope(f"c_wait{p}"):
-            core_copy(p).wait_recv()
-        c_rx[p] = c_rx[p] + c_buf[p, core]
+    def divide(p):
         (x0, z0), (x1, z1) = ORDER[2 * p], ORDER[2 * p + 1]
         other = at_plane(x0 + core * (x1 - x0), z0 + core * (z1 - z0))
         w0, w1 = (0.5 if d in HALF else 1.0 for d in ORDER[2 * p : 2 * p + 2])
@@ -304,17 +342,28 @@
         minus = jnp.zeros((8, 128), F32)
         for b in range(NB):
             minus = jnp.where(quad_b == b, ev_ref[other * 32 + yy * NB + b], minus)
-        minus = jnp.concatenate([minus, minus], 0)
+        for q in range(10):
+            rows = slice(8 * q, 8 * q + 8)
+            part = row_e[rows] - minus
+            for l in range(5):
+                lanes = slice(128 * l, 128 * l + 128)
+                factor[p, rows, lanes] = weight / (part + lane_e[:, lanes])
+
+    def finish(p):
+        with jax.named_scope(f"c_wait{p}"):
+            core_copy(p).wait_recv()
+        c_rx[p] = c_rx[p] + c_buf[p, core]
         shares = jnp.zeros((16, 128), F32)
         for q in range(5):
             rows = slice(16 * q, 16 * q + 16)
-            part = row_e[rows] - minus
             for l in range(5):
                 lanes = slice(128 * l, 128 * l + 128)
                 value = c_rx[p, rows, lanes]
-                swapped = swap_quads(c_rx[p, 16 * l : 16 * l + 16, 128 * q : 128 * q + 128])
-                lane = lane_e[:, lanes]
-                term = value * (2.0 * value - swapped) * (weight / (part + jnp.concatenate([lane, lane], 0)))
+                inner = 2.0 * value
+                if l >= q:
+                    swapped = swap_quads(c_rx[p, 16 * l : 16 * l + 16, 128 * q : 128 * q + 128])
+                    inner = inner - swapped if l == q else 2.0 * (value - swapped)
+                term = value * inner * factor[p, rows, lanes]
                 eacc[rows, lanes] += term
                 shares += term
         shares = shares[:8] + shares[8:]
@@ -322,7 +371,9 @@
         msg[...] += jnp.where(iota((4, 128), 1) == 100 + p, total, 0.0)
 
     for step in program_order():
-        if step[0] == "a":
+        if step[0] == "s":
+            take_slab(step[1])
+        elif step[0] == "a":
             _, way, delta, h = step
             wait_ring(delta, h)
             ring_copy(way, delta, h).start()
@@ -333,7 +384,7 @@
                 tree_copy(child, piece).start()
         else:
             with jax.named_scope("_".join(map(str, step))):
-                multiply(*step[1:]) if step[0] == "m" else finish(*step[1:])
+                {"m": multiply, "f": finish, "d": divide}[step[0]](*step[1:])
 
     total = eacc[...]
     lane = iota((AW, 128), 1)
@@ -362,6 +413,13 @@
     for r in range(4):
         tail = jnp.where(row == r, pltpu.roll(own, 100 - 8 * r, 1), tail)
 
+    def drain(ref, sem):
+        pltpu.make_async_copy(ref, ref, sem).wait()
+
+    drain(s_in.at[1:], s_send)
+    drain(a_buf.at[KP:], a_send)
+    drain(r_buf.at[1:], r_send)
+    drain(c_rx, c_send)
     with jax.named_scope("f_wait"):
         pltpu.make_async_copy(rx1.at[1:], rx1.at[1:], f_recv).wait()
     pairs = msg[...]
@@ -390,13 +448,6 @@
         total = total + rx2[e]
     sum_ref[...] = total
 
-    def drain(ref, sem):
-        pltpu.make_async_copy(ref, ref, sem).wait()
-
-    drain(s_in.at[1:], s_send)
-    drain(a_buf.at[KP:], a_send)
-    drain(r_buf.at[1:], r_send)
-    drain(c_rx, c_send)
     drain(rx1.at[1:], f_send)
     drain(rx2.at[1:], g_send)
 
@@ -431,6 +482,7 @@
             pltpu.VMEM((NBLK, SR, KK), BF),
             pltpu.VMEM((NPAIR, 2, SR, AW), F32),
             pltpu.VMEM((NPAIR, SR, AW), F32),
+            pltpu.VMEM((NPAIR, SR, AW), F32),
             pltpu.VMEM((SR, AW), F32),
             pltpu.VMEM((SR, 128), F32),
             pltpu.VMEM((8, AW), F32),
@@ -438,7 +490,7 @@
             pltpu.VMEM((NX * NZ, 4, 128), F32),
             pltpu.VMEM((4, 128), F32),
             pltpu.VMEM((2 * NY, 4, 128), F32),
-            dma, dma((NY, 2)), dma, dma((NY,)), dma, dma((NBLK, PIECES)), dma, dma((NPAIR,)),
+            dma, dma((NY, A_PARTS)), dma, dma((NY,)), dma, dma((NBLK, PIECES)), dma, dma((NPAIR,)),
             dma, dma, dma, dma,
         ],
         compiler_params=pltpu.CompilerParams(collective_id=0, has_side_effects=True, vmem_limit_bytes=56 * 1024 * 1024),

time: 68.8 us -> 67.5 us (0.981)
  Pallas kernels: 68 us -> 66.7 us
    pallas_call x1, Pallas kernels: 66.5 us -> 65.2 us  [on_device(): pl.pallas_call(kernel, out_shape=jax.ShapeDtypeStruct((4, 128), F32), in_...]
where the time goes in v3:
time: 67.5 us; the launch traced here: 67.3 us
  Pallas kernels  66.7 us (99%)
    pallas_call x1, Pallas kernels, on_device(): pl.pallas_call(kernel, out_shape=jax.ShapeDtypeStruct((4, 128), F32), in_...  65.2 us
    pallas_call x1, Pallas kernels, on_device(): pl.pallas_call(open_sums, out_shape=(jax.ShapeDtypeStruct((32,), F32), ja...  1.43 us

profile of v3, /device:TPU:1, one launch (start us, length us, event | category | flops | bytes accessed | tf_op | source)
XLA Modules:
  0.0 67.3 jit_solution(14740376191901611024)
XLA Ops:
  0.6 65.2 %mp2.1.sum_ref = f32[4,128]{1,0:T(4,128)} custom-call(bf16[150,640]{1,0:T(8,128)(2,1)} %x_ref.1, f32[20]{0:T(128)} %eo_ref.1, f32[1024]{0:T(1024)} %ev_ref.1), custom_call_target="tpu_custom_call" | custom-call | tf_op jit(solution)/shard_map/mp2/pallas_call | solution.py:472
  65.9 1.4 %sums.1 = (f32[32]{0:T(128)}, f32[20,20]{1,0:T(8,128)}) custom-call(f32[4,128]{1,0:T(4,128)} %mp2.1.sum_ref), custom_call_target="tpu_custom_call" | custom-call | tf_op jit(solution)/shard_map/sums/pallas_call | solution.py:499

commit v4 on v3

--- a/solution.py
+++ b/solution.py
@@ -65,6 +65,7 @@
 
 
 PLANE = sorted(range(1, NX * NZ), key=lambda e: -hops(e // NZ, e % NZ, 0))
+NEXT = [e for e in PLANE if hops(e // NZ, e % NZ, 0) == 1]
 LINE = sorted(range(1, 2 * NY), key=lambda e: -hops(0, 0, e // 2))
 
 
@@ -91,7 +92,7 @@
     for block, row in TREE.items():
         for piece, (_, t) in enumerate(row):
             arrival[block, piece] = t
-            if passed_on(block, piece):
+            if piece == 0 or passed_on(block, piece):
                 forward.append((t, ("r", block, piece)))
     forward += [(t, ("s", pos)) for pos, t in enumerate(SLABS) if pos]
     rings = {}
@@ -187,7 +188,7 @@
 def kernel(
     x_ref, eo_ref, ev_ref, sum_ref,
     a_buf, slab, s_in, s_all, r_buf, c_buf, c_rx, factor, eacc, row_e, lane_e, msg, rx1, msg2, rx2,
-    a_send, a_recv, s_send, s_recv, r_send, r_recv, c_send, c_recv, f_send, f_recv, g_send, g_recv,
+    a_send, a_recv, s_send, s_recv, r_send, r_recv, c_send, c_recv, f_send, f_recv, g_send, g_recv, hello,
 ):
     w, u = lax.axis_index("virt"), lax.axis_index("aux")
     xx, zz = w // NZ, w % NZ
@@ -200,7 +201,7 @@
         return (yy + dy) % NY * 2 + (core + dc) % 2
 
     barrier = pltpu.get_barrier_semaphore()
-    for e in PLANE:
+    for e in NEXT:
         pl.semaphore_signal(barrier, inc=1, device_id=(at_plane(e // NZ, e % NZ), u), device_id_type=MESH)
     for e in LINE:
         pl.semaphore_signal(barrier, inc=1, device_id=(w, at_line(e // 2, e % 2)), device_id_type=MESH)
@@ -217,7 +218,7 @@
         slab[n] = pack(both[:, :128]).astype(BF)
         slab[n + 1] = pack(both[:, 128:]).astype(BF)
     with jax.named_scope("barrier"):
-        pl.semaphore_wait(barrier, NX * NZ - 1 + 2 * NY - 1)
+        pl.semaphore_wait(barrier, len(NEXT) + len(LINE))
 
     def slab_copy(delta):
         return pltpu.make_async_remote_copy(
@@ -306,6 +307,8 @@
             seen.add(("r", block, piece))
             with jax.named_scope(f"r{block[0]}{block[1]}_{piece}"):
                 tree_copy(block, piece).wait_recv()
+            if piece == 0:
+                pl.semaphore_signal(hello, inc=1, device_id=(at_plane(*block), u), device_id_type=MESH)
 
     def wait_ring(delta, h):
         if ("a", delta, h) not in seen:
@@ -397,6 +400,7 @@
     rest = (summed - high.astype(F32)).astype(BF)
     packed = jnp.dot(fold, high, preferred_element_type=F32) + jnp.dot(fold, rest, preferred_element_type=F32)
     msg[...] += packed[:4]
+    pl.semaphore_wait(hello, NBLK - 1)
     for e in PLANE:
         pltpu.make_async_remote_copy(
             src_ref=msg, dst_ref=rx1.at[e], send_sem=f_send, recv_sem=f_recv,
@@ -491,7 +495,7 @@
             pltpu.VMEM((4, 128), F32),
             pltpu.VMEM((2 * NY, 4, 128), F32),
             dma, dma((NY, A_PARTS)), dma, dma((NY,)), dma, dma((NBLK, PIECES)), dma, dma((NPAIR,)),
-            dma, dma, dma, dma,
+            dma, dma, dma, dma, pltpu.SemaphoreType.REGULAR,
         ],
         compiler_params=pltpu.CompilerParams(collective_id=0, has_side_effects=True, vmem_limit_bytes=56 * 1024 * 1024),
         name="mp2",

time: 67.5 us -> 66.1 us (0.979)
  Pallas kernels: 66.7 us -> 65.3 us
    pallas_call x1, Pallas kernels: 65.2 us -> 63.8 us  [on_device(): pl.pallas_call(kernel, out_shape=jax.ShapeDtypeStruct((4, 128), F32), in_...]
where the time goes in v4:
time: 66.1 us; the launch traced here: 65.9 us
  Pallas kernels  65.3 us (99%)
    pallas_call x1, Pallas kernels, on_device(): pl.pallas_call(kernel, out_shape=jax.ShapeDtypeStruct((4, 128), F32), in_...  63.8 us
    pallas_call x1, Pallas kernels, on_device(): pl.pallas_call(open_sums, out_shape=(jax.ShapeDtypeStruct((32,), F32), ja...  1.43 us

profile of v4, /device:TPU:1, one launch (start us, length us, event | category | flops | bytes accessed | tf_op | source)
XLA Modules:
  0.0 65.9 jit_solution(7490573928532467838)
XLA Ops:
  0.6 63.8 %mp2.1.sum_ref = f32[4,128]{1,0:T(4,128)} custom-call(bf16[150,640]{1,0:T(8,128)(2,1)} %x_ref.1, f32[20]{0:T(128)} %eo_ref.1, f32[1024]{0:T(1024)} %ev_ref.1), custom_call_target="tpu_custom_call" | custom-call | tf_op jit(solution)/shard_map/mp2/pallas_call | solution.py:476
  64.5 1.4 %sums.1 = (f32[32]{0:T(128)}, f32[20,20]{1,0:T(8,128)}) custom-call(f32[4,128]{1,0:T(4,128)} %mp2.1.sum_ref), custom_call_target="tpu_custom_call" | custom-call | tf_op jit(solution)/shard_map/sums/pallas_call | solution.py:503

commit v5 on v4

--- a/solution.py
+++ b/solution.py
@@ -10,6 +10,7 @@
 F32 = jnp.float32
 
 O = 20
+VIRT = 1024
 NX, NY, NZ = 4, 8, 8
 ROWS, KP = 150, 160
 AW = 640
@@ -186,10 +187,16 @@
 
 
 def kernel(
-    x_ref, eo_ref, ev_ref, sum_ref,
-    a_buf, slab, s_in, s_all, r_buf, c_buf, c_rx, factor, eacc, row_e, lane_e, msg, rx1, msg2, rx2,
+    x_hbm, eo_hbm, ev_hbm, sum_ref, x_ref, eo_ref, ev_ref, in_sem,
+    a_buf, slab, s_in, s_all, r_buf, c_buf, c_rx, factor, eacc, row_e, lane_e, msg, rx1, msg2, rx2, gather,
     a_send, a_recv, s_send, s_recv, r_send, r_recv, c_send, c_recv, f_send, f_recv, g_send, g_recv, hello,
 ):
+    inputs = [
+        pltpu.make_async_copy(given, here, in_sem.at[n])
+        for n, (given, here) in enumerate(((x_hbm, x_ref), (eo_hbm, eo_ref), (ev_hbm, ev_ref)))
+    ]
+    for copy in inputs:
+        copy.start()
     w, u = lax.axis_index("virt"), lax.axis_index("aux")
     xx, zz = w // NZ, w % NZ
     yy, core = u // 2, u % 2
@@ -207,13 +214,14 @@
         pl.semaphore_signal(barrier, inc=1, device_id=(w, at_line(e // 2, e % 2)), device_id_type=MESH)
 
     pad = one_hot(iota((KP, ROWS), 0) == iota((KP, ROWS), 1))
+    inputs[0].wait()
     own = jnp.dot(pad, x_ref[...], preferred_element_type=F32).astype(BF)
     for n in range(0, NY, 2):
-        lane = iota((AW, 256), 1)
+        lane = iota((1, 256), 1)
         inner = lane & 127
         upper = jnp.where(inner < 40, 0, 1)
         source = (4 * n + 4 * (lane // 128) + 2 * upper + (inner & 1)) * O + (inner - 40 * upper) // 2
-        pick = one_hot((iota((AW, 256), 0) == source) & (inner < SR))
+        pick = one_hot(iota((AW, 256), 0) == jnp.where(inner < SR, source, -1))
         both = jnp.dot(own, pick, preferred_element_type=F32)
         slab[n] = pack(both[:, :128]).astype(BF)
         slab[n + 1] = pack(both[:, 128:]).astype(BF)
@@ -273,10 +281,12 @@
         own_piece(0)
 
     for first, width in ((0, 256), (256, 256), (512, 128)):
-        lane = iota((AW, width), 1) + first
+        lane = iota((1, width), 1) + first
         pick = one_hot(iota((AW, width), 0) == (lane & 31) * O + lane // 32)
         a_buf[0:KP, first : first + width] = jnp.dot(own, pick, preferred_element_type=F32).astype(BF)
 
+    inputs[1].wait()
+    inputs[2].wait()
     quad_b = iota((8, 128), 0) & 3
     for n in range(O // 2):
         top = iota((8, 128), 0) < 4
@@ -291,6 +301,8 @@
         for r in range(1, 4):
             occ = jnp.where(group == r, eo_ref[4 * n + r], occ)
         lane_e[:, 128 * n : 128 * n + 128] = occ - own_v
+    lane = iota((1, 128), 1)
+    gather[...] = one_hot(iota((AW, 128), 0) // 32 == jnp.where(lane < 5 * O, lane % O, -1))
     eacc[...] = jnp.zeros_like(eacc)
     msg[...] = jnp.zeros_like(msg)
 
@@ -390,9 +402,7 @@
                 {"m": multiply, "f": finish, "d": divide}[step[0]](*step[1:])
 
     total = eacc[...]
-    lane = iota((AW, 128), 1)
-    pick = one_hot((iota((AW, 128), 0) // 32 == lane % O) & (lane < 5 * O))
-    summed = split_dot(total, pick)
+    summed = split_dot(total, gather[...])
     row, lane = iota((SR, 128), 0), iota((SR, 128), 1)
     summed = jnp.where(row // 16 == lane // O, summed, 0.0)
     fold = one_hot(iota((8, SR), 0) == (iota((8, SR), 1) // 4 & 3))
@@ -471,14 +481,18 @@
 
 
 def on_device(three_index, eps_occ, eps_virt):
-    vmem, smem = pl.BlockSpec(memory_space=pltpu.VMEM), pl.BlockSpec(memory_space=pltpu.SMEM)
+    vmem = pl.BlockSpec(memory_space=pltpu.VMEM)
     dma = pltpu.SemaphoreType.DMA
     sums = pl.pallas_call(
         kernel,
         out_shape=jax.ShapeDtypeStruct((4, 128), F32),
-        in_specs=[vmem, smem, smem],
+        in_specs=[pl.BlockSpec(memory_space=pl.ANY)] * 3,
         out_specs=vmem,
         scratch_shapes=[
+            pltpu.VMEM((ROWS, AW), BF),
+            pltpu.SMEM((O,), F32),
+            pltpu.SMEM((VIRT,), F32),
+            dma((3,)),
             pltpu.VMEM((KK, AW), BF),
             pltpu.VMEM((NY, 2 * GR, 128), BF),
             pltpu.VMEM((NY, 2 * GR, 128), BF),
@@ -494,6 +508,7 @@
             pltpu.VMEM((NX * NZ, 4, 128), F32),
             pltpu.VMEM((4, 128), F32),
             pltpu.VMEM((2 * NY, 4, 128), F32),
+            pltpu.VMEM((AW, 128), BF),
             dma, dma((NY, A_PARTS)), dma, dma((NY,)), dma, dma((NBLK, PIECES)), dma, dma((NPAIR,)),
             dma, dma, dma, dma, pltpu.SemaphoreType.REGULAR,
         ],

time: 66.1 us -> 65.3 us (0.988)
  Pallas kernels: 65.3 us -> 64.5 us
    pallas_call x1, Pallas kernels: 63.8 us -> 63.1 us  [on_device(): pl.pallas_call(kernel, out_shape=jax.ShapeDtypeStruct((4, 128), F32), in_...]
where the time goes in v5:
time: 65.3 us; the launch traced here: 65.2 us
  Pallas kernels  64.5 us (99%)
    pallas_call x1, Pallas kernels, on_device(): pl.pallas_call(kernel, out_shape=jax.ShapeDtypeStruct((4, 128), F32), in_...  63.1 us
    pallas_call x1, Pallas kernels, on_device(): pl.pallas_call(open_sums, out_shape=(jax.ShapeDtypeStruct((32,), F32), ja...  1.43 us

profile of v5, /device:TPU:1, one launch (start us, length us, event | category | flops | bytes accessed | tf_op | source)
XLA Modules:
  0.0 65.2 jit_solution(9806053638763714439)
XLA Ops:
  0.6 63.1 %mp2.1.sum_ref = f32[4,128]{1,0:T(4,128)} custom-call(bf16[150,640]{1,0:T(8,128)(2,1)} %x_hbm.1, f32[20]{0:T(128)} %eo_hbm.1, f32[1024]{0:T(1024)} %ev_hbm.1), custom_call_target="tpu_custom_call" | custom-call | tf_op jit(solution)/shard_map/mp2/pallas_call | solution.py:486
  63.8 1.4 %sums.1 = (f32[32]{0:T(128)}, f32[20,20]{1,0:T(8,128)}) custom-call(f32[4,128]{1,0:T(4,128)} %mp2.1.sum_ref), custom_call_target="tpu_custom_call" | custom-call | tf_op jit(solution)/shard_map/sums/pallas_call | solution.py:518
